TPU v7x, 256 devices: a whole 4x4x8 slice. The times are simulated.
256 devices in a mesh: gx: 4 (over x), gy: 8 (over z), gz: 8 (over y, core).
Axes of the slice: x: 4, y: 4, z: 8, core: 2. Of those that a mesh axis runs over, the one named last changes fastest.
Arguments:
- tile_coords: int32 [3, 4096], P(None, ('gx', 'gy', 'gz')), may hold values from 0 to 31, as said below
- owner_map: int32 [4096], replicated, may hold values from 0 to 4095, as said below
- bin_tile: int32 [14848], P(('gx', 'gy', 'gz')), may hold values from 0 to 4095, as said below
- bin_count: int32 [14848], P(('gx', 'gy', 'gz')), may hold values from 0 to 2048, as said below
- part_cell: int32 [14848, 2048], P(('gx', 'gy', 'gz')), may hold values from 0 to 511
- part_offset: float32 [14848, 3, 2048], P(('gx', 'gy', 'gz')), may hold values from -0.5 to 0.5
- part_velocity: float32 [14848, 3, 2048], P(('gx', 'gy', 'gz')), may hold values from -5 to 5
- part_affine: float32 [14848, 9, 2048], P(('gx', 'gy', 'gz')), may hold values from -5 to 5
- part_mass: float32 [14848, 2048], P(('gx', 'gy', 'gz')), may hold values from 0.5 to 2
Outputs:
- grid_velocity: float32 [3, 2097152], P(None, ('gx', 'gy', 'gz'))
- pressure: float32 [2097152], P(('gx', 'gy', 'gz'))
- particle_velocity: float32 [14848, 3, 2048], P(('gx', 'gy', 'gz'))
Inputs may be any that keep to these rules, and one draw needn't show every extreme that they name: `tile_coords`: storage slot s lies on device s // 16 (device index over gx, gy, gz, slowest first). Coordinates are distinct; an active tile that shares a face with a tile stored on a device is stored on the same device or on one whose index differs by one along one mesh axis. `owner_map`: A permutation of the storage slots. `bin_tile`: the 58 bins of a device are first 32 bins whose tiles it stores itself, then 1 bins for each of the 26 offsets (dx, dy, dz) in -1..1 other than (0, 0, 0), in the order dx slowest, dz fastest, whose tiles are stored on the device at that offset of mesh indices. Bins of an offset that leads outside the mesh name some tile and hold no particles. The first bin_count slots of a bin hold its particles. Every device has a bin holding 2048.
All inputs are finite; a program needn't handle non-finite values.
Results may differ from a plain program's by a relative error of at most 0.0024.
The roundings to bfloat16 on the way count: a program that leaves them out, or rounds other values in their place, can miss the bound.
Values sent between devices are 32-bit elements; how exact they have to be, the bound alone decides.
No kernel may reach another device: no remote copies, remote signals or barrier semaphores. Data moves between devices by JAX's collectives and lax.ppermute only.
A program may use at most 128 MiB of HBM per device.

v0:
```python
import jax
import jax.numpy as jnp
from jax import lax
from jax.sharding import PartitionSpec as P

TILE = 8
TPD = 16
SELF_BINS = 32
NBR_BINS = 1
SWEEPS = 4


gravity_step = 0.5
face_steps = [(1, 0, 0), (-1, 0, 0), (0, 1, 0), (0, -1, 0), (0, 0, 1), (0, 0, -1)]
neighbour_steps = [
    (along_x, along_y, along_z)
    for along_x in (-1, 0, 1)
    for along_y in (-1, 0, 1)
    for along_z in (-1, 0, 1)
    if (along_x, along_y, along_z) != (0, 0, 0)
]


def from_behind(block, axis, distance):
    devices = range(lax.axis_size(axis))
    route = [(i - distance, i) for i in devices if i - distance in devices]
    return lax.ppermute(block, axis, route)


def deposits(offsets, velocity, affine, masses, living):
    moments = []
    for component in range(3):
        drift_part = velocity[:, component] - (
            affine[:, 3 * component] * offsets[:, 0]
            + affine[:, 3 * component + 1] * offsets[:, 1]
            + affine[:, 3 * component + 2] * offsets[:, 2]
        )
        moments.append(masses * drift_part)
    stacked = jnp.stack([masses] + moments, axis=1)
    return jnp.where(living[:, None, :], stacked, 0.0).astype(jnp.bfloat16)


def group_of(count_bins):
    return [divisor for divisor in range(1, 9) if count_bins % divisor == 0][-1]


def splat_bins(amounts, upper_index, lower_index):
    count_bins = amounts.shape[0]
    capacity = amounts.shape[2]
    group_size = group_of(count_bins)
    plane_cells = TILE * TILE
    value_type = amounts.dtype

    def splat_block(pieces):
        amount_block, upper_block, lower_block = pieces
        upper_hot = (
            upper_block[:, None, :] == lax.broadcasted_iota(jnp.int32, (1, TILE, 1), 1)
        ).astype(value_type)
        weighted = (amount_block[:, :, None, :] * upper_hot[:, None, :, :]).reshape(
            group_size, 4 * TILE, capacity
        )
        lower_hot = (
            lower_block[:, :, None] == lax.broadcasted_iota(jnp.int32, (1, 1, plane_cells), 2)
        ).astype(value_type)
        summed = jnp.einsum(
            "gap,gpl->gal",
            weighted,
            lower_hot,
            precision=lax.Precision.HIGHEST,
            preferred_element_type=jnp.float32,
        )
        return summed.reshape(group_size, 4, TILE * plane_cells)

    blocks = lax.map(
        splat_block,
        (
            amounts.reshape(count_bins // group_size, group_size, 4, capacity),
            upper_index.reshape(count_bins // group_size, group_size, capacity),
            lower_index.reshape(count_bins // group_size, group_size, capacity),
        ),
    )
    return blocks.reshape(count_bins, 4, TILE * plane_cells)


def sample_bins(tiles, upper_index, lower_index):
    count_bins = tiles.shape[0]
    capacity = upper_index.shape[1]
    group_size = group_of(count_bins)
    plane_cells = TILE * TILE

    def sample_block(pieces):
        tile_block, upper_block, lower_block = pieces
        lower_hot = (
            lower_block[:, None, :] == lax.broadcasted_iota(jnp.int32, (1, plane_cells, 1), 1)
        ).astype(jnp.float32)
        planes = jnp.einsum(
            "gul,glp->gup",
            tile_block.reshape(group_size, 3 * TILE, plane_cells),
            lower_hot,
            precision=lax.Precision.HIGHEST,
            preferred_element_type=jnp.float32,
        )
        upper_hot = (
            upper_block[:, None, :] == lax.broadcasted_iota(jnp.int32, (1, TILE, 1), 1)
        ).astype(jnp.float32)
        return jnp.sum(
            planes.reshape(group_size, 3, TILE, capacity) * upper_hot[:, None, :, :], axis=2
        )

    blocks = lax.map(
        sample_block,
        (
            tiles.reshape(count_bins // group_size, group_size, 3, TILE * plane_cells),
            upper_index.reshape(count_bins // group_size, group_size, capacity),
            lower_index.reshape(count_bins // group_size, group_size, capacity),
        ),
    )
    return blocks.reshape(count_bins, 3, capacity)


def into_slots(partials, owner_slots):
    hot_slots = (owner_slots[None, :] == lax.broadcasted_iota(jnp.int32, (TPD, 1), 0)).astype(
        jnp.float32
    )
    return jnp.dot(
        hot_slots,
        partials.reshape(partials.shape[0], -1),
        precision=lax.Precision.HIGHEST,
        preferred_element_type=jnp.float32,
    )


def from_slots(tiles_flat, slot_index):
    hot_rows = (slot_index[:, None] == lax.broadcasted_iota(jnp.int32, (1, TPD), 1)).astype(
        jnp.float32
    )
    picked = jnp.dot(
        hot_rows,
        tiles_flat.reshape(TPD, -1),
        precision=lax.Precision.HIGHEST,
        preferred_element_type=jnp.float32,
    )
    return picked.reshape(slot_index.shape[0], 3, -1)


def stack_rows(pieces):
    return tuple(
        (
            jnp.concatenate([portion[member] for portion in pieces], axis=0)
            for member in range(len(pieces[0]))
        )
    )


def take_rows(bundle, begin_row, length):
    return tuple(
        (lax.slice_in_dim(member, begin_row, begin_row + length, axis=0) for member in bundle)
    )


def bucket_rows(values, number):
    return lax.slice_in_dim(
        values, SELF_BINS + number * NBR_BINS, SELF_BINS + (number + 1) * NBR_BINS, axis=0
    )


def move_out(bundle, direction, orient):
    if direction == 0:
        return from_behind(bundle, "gx", orient)
    if direction == 1:
        return from_behind(bundle, "gy", orient)
    return from_behind(bundle, "gz", orient)


def move_back(bundle, direction, orient):
    if direction == 0:
        return from_behind(bundle, "gx", orient)
    if direction == 1:
        return from_behind(bundle, "gy", orient)
    return from_behind(bundle, "gz", orient)


def sectioned_route(buckets):
    holding = {relative: buckets[number] for number, relative in enumerate(neighbour_steps)}
    record = []
    for direction in range(3):
        for orient in (1, -1):
            leaving = [relative for relative in sorted(holding) if relative[direction] == orient]
            arrived = move_out(
                stack_rows([holding[relative] for relative in leaving]), direction, orient
            )
            remaining = {
                relative: holding[relative] for relative in holding if relative[direction] != orient
            }
            entries = []
            begin_row = 0
            for relative in leaving:
                length = holding[relative][0].shape[0]
                portion = take_rows(arrived, begin_row, length)
                begin_row = begin_row + length
                target = tuple(
                    (0 if position == direction else relative[position] for position in range(3))
                )
                if target in remaining:
                    entries.append((relative, length, target, remaining[target][0].shape[0]))
                    remaining[target] = stack_rows([remaining[target], portion])
                else:
                    entries.append((relative, length, target, 0))
                    remaining[target] = portion
            holding = remaining
            record.append((direction, orient, entries))
    own_lengths = [bucket[0].shape[0] for bucket in buckets]

    def answer(replies):
        giving = {(0, 0, 0): replies}
        for direction, orient, entries in reversed(record):
            bundle = stack_rows(
                [
                    take_rows(giving[target], offset, length)
                    for relative, length, target, offset in entries
                ]
            )
            returned = move_back(bundle, direction, -orient)
            begin_row = 0
            for relative, length, target, offset in entries:
                giving[relative] = take_rows(returned, begin_row, length)
                begin_row = begin_row + length
        return [
            take_rows(giving[relative], 0, own_lengths[number])
            for number, relative in enumerate(neighbour_steps)
        ]

    return (holding[0, 0, 0], answer)


def deliver(buckets):
    return sectioned_route(buckets)


def export_faces(values):
    return jnp.stack(
        [
            values[:, 0],
            values[:, -1],
            values[:, :, 0],
            values[:, :, -1],
            values[:, :, :, 0],
            values[:, :, :, -1],
        ],
        axis=1,
    )


def component_faces(velocity):
    return jnp.stack(
        [
            velocity[:, 0, 0],
            velocity[:, 0, -1],
            velocity[:, 1, :, 0],
            velocity[:, 1, :, -1],
            velocity[:, 2, :, :, 0],
            velocity[:, 2, :, :, -1],
        ],
        axis=1,
    )


def beside(values, face_table, neighbour_rows, facing):
    direction = facing // 2
    chosen_rows = neighbour_rows[:, facing]
    ghost_layer = jnp.where(
        (chosen_rows >= 0)[:, None, None], face_table[jnp.maximum(chosen_rows, 0), facing], 0.0
    )
    ghost_layer = jnp.expand_dims(ghost_layer, direction + 1)
    extent = values.shape[1]
    if facing % 2 == 0:
        return jnp.concatenate(
            [lax.slice_in_dim(values, 1, extent, axis=direction + 1), ghost_layer],
            axis=direction + 1,
        )
    return jnp.concatenate(
        [ghost_layer, lax.slice_in_dim(values, 0, extent - 1, axis=direction + 1)],
        axis=direction + 1,
    )


def beside_all(values, face_table, neighbour_rows):
    summed = beside(values, face_table, neighbour_rows, 0)
    for facing in range(1, 6):
        summed = summed + beside(values, face_table, neighbour_rows, facing)
    return summed


def pressure_move(bundle, direction, orient):
    if direction == 0:
        return from_behind(bundle, "gx", orient)
    if direction == 1:
        return from_behind(bundle, "gy", orient)
    return from_behind(bundle, "gz", orient)


def velocity_move(bundle, direction, orient):
    if direction == 0:
        return from_behind((bundle[0], bundle[1]), "gx", orient)
    if direction == 1:
        return from_behind((bundle[0], bundle[1]), "gy", orient)
    return from_behind((bundle[0], bundle[1]), "gz", orient)


def pressure_table(pressure):
    local_faces = export_faces(pressure).reshape(TPD, 6, TILE * TILE)
    pieces = [local_faces] + [
        pressure_move(local_faces, direction, orient)
        for direction in range(3)
        for orient in (1, -1)
    ]
    return jnp.concatenate(pieces, axis=0).reshape(7 * TPD, 6, TILE, TILE)


def velocity_table_of(local_faces, coord_values):
    face_pieces = [local_faces]
    coord_pieces = [jnp.transpose(coord_values)]
    for direction in range(3):
        for orient in (1, -1):
            got_faces, got_coords = velocity_move((local_faces, coord_values), direction, orient)
            face_pieces.append(got_faces)
            coord_pieces.append(jnp.transpose(got_coords))
    return (
        jnp.concatenate(face_pieces, axis=0).reshape(7 * TPD, 6, TILE, TILE),
        jnp.concatenate(coord_pieces, axis=0),
    )


def find_rows(coord_values, candidates):
    listing = []
    for relative in face_steps:
        wanted = coord_values + jnp.array(relative, dtype=jnp.float32)[:, None]
        matches = jnp.all(candidates[None, :, :] == jnp.transpose(wanted)[:, None, :], axis=2)
        located = jnp.any(matches, axis=1)
        position = jnp.sum(
            jnp.where(matches, lax.broadcasted_iota(jnp.int32, matches.shape, 1), 0), axis=1
        )
        listing.append(jnp.where(located, position, -1))
    return jnp.stack(listing, axis=1)


def local(
    tile_coords,
    owner_map,
    bin_tile,
    bin_count,
    part_cell,
    part_offset,
    part_velocity,
    part_affine,
    part_mass,
):
    plane_cells = TILE * TILE
    total_cells = TILE * plane_cells
    own_bins = SELF_BINS
    owner_slots = owner_map[bin_tile] % TPD
    living = lax.broadcasted_iota(jnp.int32, part_cell.shape, 1) < bin_count[:, None]
    amounts = deposits(part_offset, part_velocity, part_affine, part_mass, living)
    upper_index = part_cell // plane_cells
    lower_index = part_cell % plane_cells
    slot_values = owner_slots.astype(jnp.float32)
    partials = splat_bins(amounts, upper_index, lower_index)
    totals = into_slots(partials[:own_bins], owner_slots[:own_bins])
    buckets = [
        (bucket_rows(partials, number), bucket_rows(slot_values, number)) for number in range(26)
    ]
    arrived, answer = deliver(buckets)
    got_partials, got_slots = arrived
    got_slot_index = got_slots.astype(jnp.int32)
    totals = totals + into_slots(got_partials, got_slot_index)
    totals = totals.reshape(TPD, 4, TILE, TILE, TILE)
    masses = totals[:, 0]
    fluid_mask = masses > 0.0
    safe_mass = jnp.where(fluid_mask, masses, 1.0)
    velocity = jnp.where(fluid_mask[:, None], totals[:, 1:] / safe_mass[:, None], 0.0)
    upward = jnp.array([0.0, 1.0, 0.0], dtype=jnp.float32)
    velocity = (
        velocity
        - gravity_step * fluid_mask.astype(jnp.float32)[:, None] * upward[None, :, None, None, None]
    )
    coord_values = (tile_coords + 1).astype(jnp.float32)
    local_faces = component_faces(velocity).reshape(TPD, 6, plane_cells)
    velocity_table, candidates = velocity_table_of(local_faces, coord_values)
    neighbour_rows = find_rows(coord_values, candidates)
    diverge = 0.5 * (
        beside(velocity[:, 0], velocity_table, neighbour_rows, 0)
        - beside(velocity[:, 0], velocity_table, neighbour_rows, 1)
    )
    diverge = diverge + 0.5 * (
        beside(velocity[:, 1], velocity_table, neighbour_rows, 2)
        - beside(velocity[:, 1], velocity_table, neighbour_rows, 3)
    )
    diverge = diverge + 0.5 * (
        beside(velocity[:, 2], velocity_table, neighbour_rows, 4)
        - beside(velocity[:, 2], velocity_table, neighbour_rows, 5)
    )
    pressure = jnp.where(fluid_mask, (0.0 - diverge) / 6.0, 0.0)
    for sweep_number in range(SWEEPS - 1):
        face_table = pressure_table(pressure)
        pressure = jnp.where(
            fluid_mask, (beside_all(pressure, face_table, neighbour_rows) - diverge) / 6.0, 0.0
        )
    face_table = pressure_table(pressure)
    gradient = jnp.stack(
        [
            0.5
            * (
                beside(pressure, face_table, neighbour_rows, 2 * component)
                - beside(pressure, face_table, neighbour_rows, 2 * component + 1)
            )
            for component in range(3)
        ],
        axis=1,
    )
    velocity = jnp.where(fluid_mask[:, None], velocity - gradient, 0.0)
    tiles_flat = velocity.reshape(TPD, 3, total_cells)
    flat_velocity = jnp.transpose(tiles_flat, (1, 0, 2)).reshape(3, TPD * total_cells)
    near_values = sample_bins(
        from_slots(tiles_flat, owner_slots[:own_bins]),
        upper_index[:own_bins],
        lower_index[:own_bins],
    )
    replies = (from_slots(tiles_flat, got_slot_index),)
    remote_tiles = stack_rows(answer(replies))[0]
    remote = sample_bins(remote_tiles, upper_index[own_bins:], lower_index[own_bins:])
    sampled = jnp.concatenate([near_values, remote], axis=0)
    particle_velocity = jnp.where(living[:, None, :], sampled, 0.0)
    return (flat_velocity, pressure.reshape(-1), particle_velocity)


def solution(mesh):
    placed = (
        P(None, ("gx", "gy", "gz")),
        P(),
        P(("gx", "gy", "gz")),
        P(("gx", "gy", "gz")),
        P(("gx", "gy", "gz"), None),
        P(("gx", "gy", "gz"), None, None),
        P(("gx", "gy", "gz"), None, None),
        P(("gx", "gy", "gz"), None, None),
        P(("gx", "gy", "gz"), None),
    )
    return jax.shard_map(
        local,
        mesh=mesh,
        in_specs=placed,
        out_specs=(
            P(None, ("gx", "gy", "gz")),
            P(("gx", "gy", "gz")),
            P(("gx", "gy", "gz"), None, None),
        ),
        check_vma=False,
    )
```

profile of v0, /device:TPU:116, one launch (start us, length us, event | category | flops | bytes accessed | tf_op | source)
XLA Modules:
  0.0 545.5 jit_solution(4980197705691017671)
XLA Ops:
  7.2 5.0 collective-permute-start.14
  29.0 3.5 fusion.17
  32.4 73.7 %while.30 = (s32[]{:T(128)}, f32[29,2,4,512]{3,2,1,0:T(4,128)}, bf16[29,2,4,2048]{3,2,1,0:T(4,128)(2,1)}, s32[29,2,2048]{2,1,0:T(2,128)}, s32[29,2,2048]{2,1,0:T(2,128)}, /*index=5*/s32[]{:T(128)}) while((s32[]{:T(128)}, f32[29,2,4,512]{3,2,1,0:T(4,128)}, bf16[29,2,4,2048]{3,2,1,0:T(4,128)(2,1)}, s32[29,2,2048]{2,1,0:T(2,128)}, ...), condition=%wide.region_1.2_spmd, body=%wide.region_0.1_spmd.sunk | while | flops 17235968 | bytes 410189 | solution.py:74
  113.2 3.4 collective-permute-start
  119.3 5.7 %concatenate.290 = f32[9]{0:T(128)S(1)} concatenate(f32[1]{0:T(128)} %get-tuple-element.305, f32[1]{0:T(128)} %get-tuple-element.296, f32[1]{0:T(128)} %get-tuple-element.287, f32[1]{0:T(128)} %get-tuple-element.304, f32[1]{0:T(128)} %get-tuple-element.295, f32[1]{0:T(128)} %get-tuple-element.286, f32[1]{0:T(128)} %get-tuple-element.303, f32[1]{0:T(128)} %get-tuple-element.294, ...), dimensions={0} | concatenate | bytes 72 | tf_op jit(solution)/shard_map/concatenate | solution.py:149
  127.0 5.8 %concatenate.289 = f32[9]{0:T(128)S(1)} concatenate(f32[1]{0:T(128)} %get-tuple-element.308, f32[1]{0:T(128)} %get-tuple-element.299, f32[1]{0:T(128)} %get-tuple-element.290, f32[1]{0:T(128)} %get-tuple-element.307, f32[1]{0:T(128)} %get-tuple-element.298, f32[1]{0:T(128)} %get-tuple-element.289, f32[1]{0:T(128)} %get-tuple-element.306, f32[1]{0:T(128)} %get-tuple-element.297, ...), dimensions={0} | concatenate | bytes 72 | tf_op jit(solution)/shard_map/concatenate | solution.py:149
  132.7 5.1 collective-permute-start.2
  157.0 3.4 collective-permute-start.6
  168.2 5.4 collective-permute-start.8
  175.6 5.5 %collective-permute-done.9 = f32[9,4,512]{2,1,0:T(4,128)S(1)} collective-permute-done((f32[9,4,512]{2,1,0:T(4,128)S(1)}, f32[9,4,512]{2,1,0:T(4,128)S(1)}, u32[]{:S(2)}, u32[]{:S(2)}) %collective-permute-start.9) | collective-permute-done | bytes 73760 | tf_op jit(solution)/shard_map/ppermute | solution.py:27
  183.6 3.6 collective-permute-start.11
  196.1 3.6 collective-permute-start.19
  201.7 3.9 collective-permute-start.21
  208.7 3.5 collective-permute-start.23
  261.9 3.4 copy.331
  306.4 3.9 collective-permute-start.32
  324.9 3.4 copy.343
  369.4 3.8 collective-permute-start.38
  424.0 4.5 collective-permute-start.44
  480.1 5.1 collective-permute-start.50
  487.5 5.9 %collective-permute-done.51 = f32[9,3,512]{2,1,0:T(4,128)S(1)} collective-permute-done((f32[9,3,512]{2,1,0:T(4,128)S(1)}, f32[9,3,512]{2,1,0:T(4,128)S(1)}, u32[]{:S(2)}, u32[]{:S(2)}) %collective-permute-start.51) | collective-permute-done | bytes 55328 | tf_op jit(solution)/shard_map/ppermute | solution.py:27
  493.4 3.6 collective-permute-start.52
  503.0 11.3 %while.31 = (s32[]{:T(128)}, f32[4,8,3,2048]{3,1,0,2:T(8,128)}, f32[4,8,3,512]{3,1,2,0:T(8,128)S(1)}, s32[4,8,2048]{2,1,0:T(8,128)S(1)}, s32[4,8,2048]{2,1,0:T(8,128)S(1)}, /*index=5*/s32[]{:T(128)}) while((s32[]{:T(128)}, f32[4,8,3,2048]{3,1,0,2:T(8,128)}, f32[4,8,3,512]{3,1,2,0:T(8,128)S(1)}, s32[4,8,2048]{2,1,0:T(8,128)S(1)}, ...), condition=%wide.region_22.23_spmd, body=%wide.region_20.22_spmd.sunk | while | flops 304037888 | bytes 2376269 | solution.py:110
  515.9 27.9 %while.32 = (s32[]{:T(128)}, f32[13,2,3,2048]{3,2,1,0:T(4,128)S(1)}, f32[13,2,3,512]{3,2,1,0:T(4,128)}, s32[13,2,2048]{2,1,0:T(2,128)}, s32[13,2,2048]{2,1,0:T(2,128)}, /*index=5*/s32[]{:T(128)}) while((s32[]{:T(128)}, f32[13,2,3,2048]{3,2,1,0:T(4,128)S(1)}, f32[13,2,3,512]{3,2,1,0:T(4,128)}, s32[13,2,2048]{2,1,0:T(2,128)}, ...), condition=%wide.region_25.26_spmd, body=%wide.region_23.25_spmd.sunk | while | flops 76009472 | bytes 602193 | solution.py:110
  (763 shorter events, 450.9 us)
Async XLA Ops:
  1.3 153.3 %collective-permute-start.12 = (f32[3,16]{1,0:T(4,128)S(1)}, f32[3,16]{1,0:T(4,128)S(1)}, u32[]{:S(2)}, u32[]{:S(2)}) collective-permute-start(f32[3,16]{1,0:T(4,128)S(1)} %get-tuple-element.275), channel_id=1, source_target_pairs={{0,64},{64,128},{128,192},{1,65},{65,129},{129,193},{2,66},{66,130... | collective-permute-start | bytes 584 | tf_op jit(solution)/shard_map/ppermute | solution.py:27
  4.4 152.5 %collective-permute-start.13 = (f32[3,16]{1,0:T(4,128)S(1)}, f32[3,16]{1,0:T(4,128)S(1)}, u32[]{:S(2)}, u32[]{:S(2)}) collective-permute-start(f32[3,16]{1,0:T(4,128)S(1)} %get-tuple-element.275), channel_id=1, source_target_pairs={{64,0},{128,64},{192,128},{65,1},{129,65},{193,129},{66,2},{130,66... | collective-permute-start | bytes 584 | tf_op jit(solution)/shard_map/ppermute | solution.py:27
  7.2 153.2 %collective-permute-start.14 = (f32[3,16]{1,0:T(4,128)S(1)}, f32[3,16]{1,0:T(4,128)S(1)}, u32[]{:S(2)}, u32[]{:S(2)}) collective-permute-start(f32[3,16]{1,0:T(4,128)S(1)} %get-tuple-element.275), channel_id=1, source_target_pairs={{0,8},{8,16},{16,24},{24,32},{32,40},{40,48},{48,56},{1,9},{9,17},... | collective-permute-start | bytes 584 | tf_op jit(solution)/shard_map/ppermute | solution.py:27
  12.2 150.6 %collective-permute-start.15 = (f32[3,16]{1,0:T(4,128)S(1)}, f32[3,16]{1,0:T(4,128)S(1)}, u32[]{:S(2)}, u32[]{:S(2)}) collective-permute-start(f32[3,16]{1,0:T(4,128)S(1)} %get-tuple-element.275), channel_id=1, source_target_pairs={{8,0},{16,8},{24,16},{32,24},{40,32},{48,40},{56,48},{9,1},{17,9},... | collective-permute-start | bytes 584 | tf_op jit(solution)/shard_map/ppermute | solution.py:27
  15.7 97.5 %collective-permute-start.1 = (f32[9]{0:T(128)S(1)}, f32[9]{0:T(128)S(1)}, u32[]{:S(2)}, u32[]{:S(2)}) collective-permute-start(f32[9]{0:T(128)S(1)} %get-tuple-element.309), channel_id=1, source_target_pairs={{64,0},{128,64},{192,128},{65,1},{129,65},{193,129},{66,2},{130,66... | collective-permute-start | bytes 116 | tf_op jit(solution)/shard_map/ppermute | solution.py:27
  150.1 12.8 %collective-permute-start.16 = (f32[3,16]{1,0:T(4,128)S(1)}, f32[3,16]{1,0:T(4,128)S(1)}, u32[]{:S(2)}, u32[]{:S(2)}) collective-permute-start(f32[3,16]{1,0:T(4,128)S(1)} %get-tuple-element.275), channel_id=1, source_target_pairs={{0,1},{1,2},{2,3},{3,4},{4,5},{5,6},{6,7},{8,9},{9,10},{10,11},{11... | collective-permute-start | bytes 584 | tf_op jit(solution)/shard_map/ppermute | solution.py:27
  193.9 14.8 %collective-permute-start.18 = (f32[16,6,64]{0,2,1:T(8,128)}, f32[16,6,64]{0,2,1:T(8,128)S(1)}, u32[]{:S(2)}, u32[]{:S(2)}) collective-permute-start(f32[16,6,64]{0,2,1:T(8,128)} %constant_dynamic-update-slice_fusion.35), channel_id=1, source_target_pairs={{0,64},{64,128},{128,192},{1,65},{65,129},{129,193},{2,66},{66,130... | collective-permute-start | bytes 73736 | tf_op jit(solution)/shard_map/ppermute | solution.py:27
  196.1 17.8 %collective-permute-start.19 = (f32[16,6,64]{0,2,1:T(8,128)}, f32[16,6,64]{0,2,1:T(8,128)}, u32[]{:S(2)}, u32[]{:S(2)}) collective-permute-start(f32[16,6,64]{0,2,1:T(8,128)} %constant_dynamic-update-slice_fusion.35), channel_id=1, source_target_pairs={{64,0},{128,64},{192,128},{65,1},{129,65},{193,129},{66,2},{130,66... | collective-permute-start | bytes 73736 | tf_op jit(solution)/shard_map/ppermute | solution.py:27
  199.8 14.1 %collective-permute-start.20 = (f32[16,6,64]{0,2,1:T(8,128)}, f32[16,6,64]{0,2,1:T(8,128)}, u32[]{:S(2)}, u32[]{:S(2)}) collective-permute-start(f32[16,6,64]{0,2,1:T(8,128)} %constant_dynamic-update-slice_fusion.35), channel_id=1, source_target_pairs={{0,8},{8,16},{16,24},{24,32},{32,40},{40,48},{48,56},{1,9},{9,17},... | collective-permute-start | bytes 73736 | tf_op jit(solution)/shard_map/ppermute | solution.py:27
  201.7 12.2 %collective-permute-start.21 = (f32[16,6,64]{0,2,1:T(8,128)}, f32[16,6,64]{0,2,1:T(8,128)}, u32[]{:S(2)}, u32[]{:S(2)}) collective-permute-start(f32[16,6,64]{0,2,1:T(8,128)} %constant_dynamic-update-slice_fusion.35), channel_id=1, source_target_pairs={{8,0},{16,8},{24,16},{32,24},{40,32},{48,40},{56,48},{9,1},{17,9},... | collective-permute-start | bytes 73736 | tf_op jit(solution)/shard_map/ppermute | solution.py:27
  238.5 14.2 %collective-permute-start.24 = (f32[16,6,64]{0,2,1:T(8,128)S(1)}, f32[16,6,64]{0,2,1:T(8,128)S(1)}, u32[]{:S(2)}, u32[]{:S(2)}) collective-permute-start(f32[16,6,64]{0,2,1:T(8,128)S(1)} %constant_dynamic-update-slice_fusion.41), channel_id=1, source_target_pairs={{0,64},{64,128},{128,192},{1,65},{65,129},{129,193},{2,66},{66,130... | collective-permute-start | bytes 73736 | tf_op jit(solution)/shard_map/ppermute | solution.py:27
  241.4 15.4 %collective-permute-start.25 = (f32[16,6,64]{0,2,1:T(8,128)S(1)}, f32[16,6,64]{0,2,1:T(8,128)S(1)}, u32[]{:S(2)}, u32[]{:S(2)}) collective-permute-start(f32[16,6,64]{0,2,1:T(8,128)S(1)} %constant_dynamic-update-slice_fusion.41), channel_id=1, source_target_pairs={{64,0},{128,64},{192,128},{65,1},{129,65},{193,129},{66,2},{130,66... | collective-permute-start | bytes 73736 | tf_op jit(solution)/shard_map/ppermute | solution.py:27
  244.4 12.4 %collective-permute-start.26 = (f32[16,6,64]{0,2,1:T(8,128)S(1)}, f32[16,6,64]{0,2,1:T(8,128)S(1)}, u32[]{:S(2)}, u32[]{:S(2)}) collective-permute-start(f32[16,6,64]{0,2,1:T(8,128)S(1)} %constant_dynamic-update-slice_fusion.41), channel_id=1, source_target_pairs={{0,8},{8,16},{16,24},{24,32},{32,40},{40,48},{48,56},{1,9},{9,17},... | collective-permute-start | bytes 73736 | tf_op jit(solution)/shard_map/ppermute | solution.py:27
  300.6 14.5 %collective-permute-start.30 = (f32[16,6,64]{0,2,1:T(8,128)S(1)}, f32[16,6,64]{0,2,1:T(8,128)S(1)}, u32[]{:S(2)}, u32[]{:S(2)}) collective-permute-start(f32[16,6,64]{0,2,1:T(8,128)S(1)} %constant_dynamic-update-slice_fusion.47), channel_id=1, source_target_pairs={{0,64},{64,128},{128,192},{1,65},{65,129},{129,193},{2,66},{66,130... | collective-permute-start | bytes 73736 | tf_op jit(solution)/shard_map/ppermute | solution.py:27
  303.5 15.3 %collective-permute-start.31 = (f32[16,6,64]{0,2,1:T(8,128)S(1)}, f32[16,6,64]{0,2,1:T(8,128)S(1)}, u32[]{:S(2)}, u32[]{:S(2)}) collective-permute-start(f32[16,6,64]{0,2,1:T(8,128)S(1)} %constant_dynamic-update-slice_fusion.47), channel_id=1, source_target_pairs={{64,0},{128,64},{192,128},{65,1},{129,65},{193,129},{66,2},{130,66... | collective-permute-start | bytes 73736 | tf_op jit(solution)/shard_map/ppermute | solution.py:27
  306.4 12.4 %collective-permute-start.32 = (f32[16,6,64]{0,2,1:T(8,128)S(1)}, f32[16,6,64]{0,2,1:T(8,128)S(1)}, u32[]{:S(2)}, u32[]{:S(2)}) collective-permute-start(f32[16,6,64]{0,2,1:T(8,128)S(1)} %constant_dynamic-update-slice_fusion.47), channel_id=1, source_target_pairs={{0,8},{8,16},{16,24},{24,32},{32,40},{40,48},{48,56},{1,9},{9,17},... | collective-permute-start | bytes 73736 | tf_op jit(solution)/shard_map/ppermute | solution.py:27
  363.5 15.1 %collective-permute-start.36 = (f32[16,6,64]{0,2,1:T(8,128)S(1)}, f32[16,6,64]{0,2,1:T(8,128)S(1)}, u32[]{:S(2)}, u32[]{:S(2)}) collective-permute-start(f32[16,6,64]{0,2,1:T(8,128)S(1)} %constant_dynamic-update-slice_fusion.53), channel_id=1, source_target_pairs={{0,64},{64,128},{128,192},{1,65},{65,129},{129,193},{2,66},{66,130... | collective-permute-start | bytes 73736 | tf_op jit(solution)/shard_map/ppermute | solution.py:27
  366.4 16.0 %collective-permute-start.37 = (f32[16,6,64]{0,2,1:T(8,128)S(1)}, f32[16,6,64]{0,2,1:T(8,128)S(1)}, u32[]{:S(2)}, u32[]{:S(2)}) collective-permute-start(f32[16,6,64]{0,2,1:T(8,128)S(1)} %constant_dynamic-update-slice_fusion.53), channel_id=1, source_target_pairs={{64,0},{128,64},{192,128},{65,1},{129,65},{193,129},{66,2},{130,66... | collective-permute-start | bytes 73736 | tf_op jit(solution)/shard_map/ppermute | solution.py:27
  369.4 13.0 %collective-permute-start.38 = (f32[16,6,64]{0,2,1:T(8,128)S(1)}, f32[16,6,64]{0,2,1:T(8,128)S(1)}, u32[]{:S(2)}, u32[]{:S(2)}) collective-permute-start(f32[16,6,64]{0,2,1:T(8,128)S(1)} %constant_dynamic-update-slice_fusion.53), channel_id=1, source_target_pairs={{0,8},{8,16},{16,24},{24,32},{32,40},{40,48},{48,56},{1,9},{9,17},... | collective-permute-start | bytes 73736 | tf_op jit(solution)/shard_map/ppermute | solution.py:27
  418.2 18.3 %collective-permute-start.42 = (f32[16,6,64]{0,2,1:T(8,128)}, f32[16,6,64]{0,2,1:T(8,128)}, u32[]{:S(2)}, u32[]{:S(2)}) collective-permute-start(f32[16,6,64]{0,2,1:T(8,128)} %constant_dynamic-update-slice_fusion.59), channel_id=1, source_target_pairs={{0,64},{64,128},{128,192},{1,65},{65,129},{129,193},{2,66},{66,130... | collective-permute-start | bytes 73736 | tf_op jit(solution)/shard_map/ppermute | solution.py:27
  421.1 18.9 %collective-permute-start.43 = (f32[16,6,64]{0,2,1:T(8,128)}, f32[16,6,64]{0,2,1:T(8,128)}, u32[]{:S(2)}, u32[]{:S(2)}) collective-permute-start(f32[16,6,64]{0,2,1:T(8,128)} %constant_dynamic-update-slice_fusion.59), channel_id=1, source_target_pairs={{64,0},{128,64},{192,128},{65,1},{129,65},{193,129},{66,2},{130,66... | collective-permute-start | bytes 73736 | tf_op jit(solution)/shard_map/ppermute | solution.py:27
  424.0 15.9 %collective-permute-start.44 = (f32[16,6,64]{0,2,1:T(8,128)}, f32[16,6,64]{0,2,1:T(8,128)}, u32[]{:S(2)}, u32[]{:S(2)}) collective-permute-start(f32[16,6,64]{0,2,1:T(8,128)} %constant_dynamic-update-slice_fusion.59), channel_id=1, source_target_pairs={{0,8},{8,16},{16,24},{24,32},{32,40},{40,48},{48,56},{1,9},{9,17},... | collective-permute-start | bytes 73736 | tf_op jit(solution)/shard_map/ppermute | solution.py:27
  428.5 11.4 %collective-permute-start.45 = (f32[16,6,64]{0,2,1:T(8,128)}, f32[16,6,64]{0,2,1:T(8,128)}, u32[]{:S(2)}, u32[]{:S(2)}) collective-permute-start(f32[16,6,64]{0,2,1:T(8,128)} %constant_dynamic-update-slice_fusion.59), channel_id=1, source_target_pairs={{8,0},{16,8},{24,16},{32,24},{40,32},{48,40},{56,48},{9,1},{17,9},... | collective-permute-start | bytes 73736 | tf_op jit(solution)/shard_map/ppermute | solution.py:27
  499.8 15.4 %collective-permute-start.53 = (f32[9,3,512]{2,1,0:T(4,128)S(1)}, f32[9,3,512]{2,1,0:T(4,128)S(1)}, u32[]{:S(2)}, u32[]{:S(2)}) collective-permute-start(f32[9,3,512]{2,1,0:T(4,128)S(1)} %get-tuple-element.225), channel_id=1, source_target_pairs={{64,0},{128,64},{192,128},{65,1},{129,65},{193,129},{66,2},{130,66... | collective-permute-start | bytes 165896 | tf_op jit(solution)/shard_map/ppermute | solution.py:27
  (83 other events, 1016.3 us)
where the time goes:
time: 557 us; the launch traced here: 546 us
  local copies, waits for them, and re-layouts  272 us (49%)
  starting transfers between devices  161 us (29%)
  other arithmetic  51.3 us (9%)
  waiting for transfers between devices  33 us (6%)
  matrix products  24.5 us (4%)
    ppermute x54, starting transfers between devices, from_behind(): return lax.ppermute(block, axis, route)  161 us
    gather x30, local copies, waits for them, and re-layouts, beside(): face_table[jnp.maximum(chosen_rows, 0), facing]  78.2 us
    ppermute x54, waiting for transfers between devices, from_behind(): return lax.ppermute(block, axis, route)  33 us
    select_n x24, local copies, waits for them, and re-layouts, beside(): jnp.where((chosen_rows >= 0)[:, None, None], face_table[jnp.maximum(chose...  23 us
    mul x29, local copies, waits for them, and re-layouts, splat_block(): amount_block[:, :, None, :] * upper_hot[:, None, :, :]  22.5 us
    select_n x24, other arithmetic, beside(): jnp.where((chosen_rows >= 0)[:, None, None], face_table[jnp.maximum(chose...  21.4 us
    eq x29, local copies, waits for them, and re-layouts, splat_block(): lower_block[:, :, None]  21.4 us
    dynamic_update_slice x29, local copies, waits for them, and re-layouts, splat_bins(): lax.map(splat_block, (amounts.reshape(count_bins // group_size, group_siz...  17.6 us
  transfers between devices with their start and end apart: 54, of which 16 were waited for; matrix products, arithmetic and copies ran while one was open for 26% of the time, Pallas kernels for 0%

commit v1 on v0

v1 whole, which is shorter than its diff:
```python
import jax
import jax.numpy as jnp
from jax import lax
from jax.experimental import pallas as pl
from jax.experimental.pallas import tpu as pltpu
from jax.sharding import PartitionSpec as P

TPD = 16
OWN_BINS = 32
NBR_BINS = 26
BINS = OWN_BINS + NBR_BINS
PPT = 2048
CELLS = 512
LANES = 128
UPPER = CELLS // LANES
REC = 16
GROUP = 9
META = GROUP * REC
PAYLOAD = META + 16
SWEEPS = 4
AXES = ("gx", "gy", "gz")
face_codes = (4096, -4096, 64, -64, 1, -1)


def ring(block, axis, distance):
    size = lax.axis_size(axis)
    return lax.ppermute(block, axis, [(i, (i + distance) % size) for i in range(size)])


def swap(block, axis, which):
    size = lax.axis_size(axis)
    pairs = [(i, ((i + which) ^ 1) - which) for i in range(size)]
    return lax.ppermute(block, axis, [(i, j % size) for i, j in pairs])


def scalars():
    return pl.BlockSpec(memory_space=pltpu.SMEM)


def held():
    return pl.BlockSpec(memory_space=pltpu.VMEM)


def near(values):
    return pltpu.with_memory_space_constraint(values, pltpu.VMEM)


def array(*shape, dtype=jnp.float32):
    return pltpu.VMEM(shape, dtype)


def call(body, name, args, outs, flops=2_000_000, **extra):
    if "grid" not in extra:
        args = [near(arg) for arg in args]
        extra["in_specs"] = [held() for _ in args]
        extra["out_specs"] = tuple(held() for _ in outs) if isinstance(outs, tuple) else held()
    return pl.pallas_call(
        body,
        out_shape=outs,
        name=name,
        cost_estimate=pl.CostEstimate(flops=flops, transcendentals=0, bytes_accessed=500_000),
        **extra,
    )(*args)


def upper_and_hot(cell_ref, row, count):
    cells = cell_ref[row : row + 1, :]
    living = lax.broadcasted_iota(jnp.int32, (1, PPT), 1) < count
    upper = jnp.where(living, cells >> 7, -1)
    lower = cells & (LANES - 1)
    hot = (lax.broadcasted_iota(jnp.int32, (LANES, PPT), 0) == lower).astype(jnp.bfloat16)
    return upper, hot


def store_deposits(off, vel, aff, mass, amounts):
    masses = mass[...]
    amounts[0] = masses.astype(jnp.bfloat16).astype(jnp.float32)
    for a in range(3):
        drift = vel[a] - (aff[3 * a] * off[0] + aff[3 * a + 1] * off[1] + aff[3 * a + 2] * off[2])
        amounts[a + 1] = (masses * drift).astype(jnp.bfloat16).astype(jnp.float32)


def splat_row(cell, amounts, row, count):
    upper, hot = upper_and_hot(cell, row, count)
    position = lax.broadcasted_iota(jnp.int32, (8, PPT), 0)
    first = position == upper
    second = position == jnp.where(upper < 0, -1, upper + UPPER)
    halves = []
    for pair in range(2):
        one = amounts[2 * pair, row : row + 1, :]
        two = amounts[2 * pair + 1, row : row + 1, :]
        halves.append(jnp.where(first, one, jnp.where(second, two, 0.0)))
    weighted = jnp.concatenate(halves, axis=0).astype(jnp.bfloat16)
    return lax.dot_general(
        weighted, hot, (((1,), (1,)), ((), ())), preferred_element_type=jnp.float32
    )


def particle_specs(start):
    return [
        pl.BlockSpec((8, PPT), lambda i: (i + start, 0)),
        pl.BlockSpec((3, 8, PPT), lambda i: (0, i + start, 0)),
        pl.BlockSpec((3, 8, PPT), lambda i: (0, i + start, 0)),
        pl.BlockSpec((9, 8, PPT), lambda i: (0, i + start, 0)),
        pl.BlockSpec((8, PPT), lambda i: (i + start, 0)),
    ]


def splat_own(counts, slots, parts, start, blocks):
    def body(counts, slots, cell, off, vel, aff, mass, acc, amounts):
        @pl.when(pl.program_id(0) == 0)
        def _():
            acc[...] = jnp.zeros_like(acc)

        store_deposits(off, vel, aff, mass, amounts)
        base = (pl.program_id(0) + start) * 8
        summed = [splat_row(cell, amounts, row, counts[base + row]) for row in range(8)]
        for row in range(8):
            place = pl.multiple_of(slots[base + row] * REC, REC)
            acc[pl.ds(place, REC), :] += summed[row]

    return call(
        body,
        "splat_own",
        (counts, slots, *parts),
        array(TPD * REC, LANES),
        flops=blocks * 8 * 2_000_000,
        grid=(blocks,),
        in_specs=[scalars(), scalars()] + particle_specs(start),
        out_specs=held(),
        scratch_shapes=[pltpu.VMEM((4, 8, PPT), jnp.float32)],
    )


def splat_nbr(tile_coords, owner_map, bin_tile, counts, parts):
    first_block = OWN_BINS // 8
    blocks = -(-NBR_BINS // 8)
    last = NBR_BINS - 8 * (blocks - 1)

    def body(coords, owners, bin_tile, counts, cell, off, vel, aff, mass, *rest):
        slots, code_row, code_column, slot_rows, below, middle, above, rec, amounts = rest
        step = pl.program_id(0)

        @pl.when(step == 0)
        def _():
            for number in range(BINS):
                slots[number] = owners[bin_tile[number]] & (TPD - 1)
            for number in range(NBR_BINS):
                value = slots[OWN_BINS + number].astype(jnp.float32)
                slot_rows[number : number + 1, :] = jnp.full((1, LANES), value, jnp.float32)
            turn_of = lax.broadcasted_iota(jnp.int32, (8, LANES), 1) & (TPD - 1)
            row_of = lax.broadcasted_iota(jnp.int32, (TPD, LANES), 0)
            along, down = jnp.zeros((8, LANES), jnp.int32), jnp.zeros((TPD, LANES), jnp.int32)
            for t in range(TPD):
                code = (coords[0, t] + 1) * 4096 + (coords[1, t] + 1) * 64 + coords[2, t] + 1
                along = jnp.where(turn_of == t, code, along)
                down = jnp.where(row_of == t, code, down)
            code_row[...] = along.astype(jnp.float32)
            code_column[...] = down.astype(jnp.float32)

        store_deposits(off, vel, aff, mass, amounts)

        def splat(rows):
            for row in range(rows):
                number = step * 8 + row
                rec[pl.ds(pl.multiple_of(number * REC, REC), REC), :] = splat_row(
                    cell, amounts, row, counts[OWN_BINS + number]
                )

        @pl.when(step < blocks - 1)
        def _():
            splat(8)

        @pl.when(step == blocks - 1)
        def _():
            splat(last)
            for out, begin in ((below, 0), (above, 17)):
                out[0:META, :] = rec[begin * REC : (begin + GROUP) * REC, :]
                out[META : META + GROUP, :] = slot_rows[begin : begin + GROUP, :]
                out[META + GROUP : META + GROUP + 1, :] = code_row[0:1, :]
                out[META + GROUP + 1 : PAYLOAD, :] = jnp.zeros((6, LANES), jnp.float32)
            middle[...] = rec[GROUP * REC : 17 * REC, :]

    return call(
        body,
        "splat_nbr",
        (tile_coords, owner_map, bin_tile, counts, *parts),
        (
            jax.ShapeDtypeStruct((BINS,), jnp.int32),
            array(8, LANES),
            array(TPD, LANES),
            array(32, LANES),
            array(PAYLOAD, LANES),
            array(8 * REC, LANES),
            array(PAYLOAD, LANES),
        ),
        flops=NBR_BINS * 2_000_000,
        grid=(blocks,),
        in_specs=[scalars()] * 4 + particle_specs(first_block),
        out_specs=(scalars(),) + (held(),) * 6,
        scratch_shapes=[
            pltpu.VMEM((NBR_BINS * REC, LANES), jnp.float32),
            pltpu.VMEM((4, 8, PPT), jnp.float32),
        ],
    )


middle_steps = [(b, c) for b in (-1, 0, 1) for c in (-1, 0, 1) if (b, c) != (0, 0)]


def mid_of(dy, dz):
    return ("mid", middle_steps.index((dy, dz)))


def y_sources(orient):
    listing = [mid_of(orient, dz) for dz in (-1, 0, 1)]
    for arrived in ("xp", "xm"):
        listing += [(arrived, (orient + 1) * 3 + dz + 1) for dz in (-1, 0, 1)]
    return listing


def z_sources(orient):
    listing = [mid_of(0, orient)]
    listing += [(arrived, 3 + orient + 1) for arrived in ("xp", "xm")]
    for arrived in ("yp", "ym"):
        listing += [(arrived, 3 * group + orient + 1) for group in range(3)]
    return listing


consumed = (
    [("zp", n) for n in range(9)]
    + [("zm", n) for n in range(9)]
    + [("yp", 3 * g + 1) for g in range(3)]
    + [("ym", 3 * g + 1) for g in range(3)]
    + [("xp", 4), ("xm", 4)]
)


def y_reply_sources(sign):
    local, offset = (18, 3) if sign > 0 else (21, 6)
    listing = []
    for g in range(3):
        listing += [("zm", offset + g), ("rec", local + g), ("zp", offset + g)]
    return listing


def x_reply_sources(sign):
    group = 1 if sign > 0 else 2
    local = ("rec", 24 if sign > 0 else 25)
    return (
        [("ym", 3 * group + n) for n in range(3)]
        + [("zm", group), local, ("zp", group)]
        + [("yp", 3 * group + n) for n in range(3)]
    )


final_sources = (
    [("xm", n) for n in range(9)]
    + [("ym", n) for n in range(3)]
    + [("zm", 0), ("zp", 0)]
    + [("yp", n) for n in range(3)]
    + [("xp", n) for n in range(9)]
)


def record(ref, number):
    return ref[number * REC : (number + 1) * REC, :]


def slot_row(refs, source, slot_rows):
    name, number = source
    if name == "mid":
        return slot_rows[GROUP + number : GROUP + number + 1, :]
    return refs[name][META + number : META + number + 1, :]


def forward(names, buffers, slot_rows, code_row, sources, title):
    def body(*refs):
        kept = dict(zip(names, refs))
        slots, codes = refs[len(names)], refs[len(names) + 1]
        for out, listing in zip(refs[len(names) + 2 :], sources):
            for number, source in enumerate(listing):
                out[number * REC : (number + 1) * REC, :] = record(kept[source[0]], source[1])
                out[META + number : META + number + 1, :] = slot_row(kept, source, slots)
            out[META + GROUP : META + GROUP + 1, :] = codes[0:1, :]
            out[META + GROUP + 1 : PAYLOAD, :] = jnp.zeros((6, LANES), jnp.float32)

    payload = array(PAYLOAD, LANES)
    return call(body, title, (*buffers, slot_rows, code_row), (payload, payload))


def reply(names, buffers, sources, title):
    def body(*refs):
        kept = dict(zip(names, refs))
        for out, listing in zip(refs[len(names) :], sources):
            for number, source in enumerate(listing):
                out[number * REC : (number + 1) * REC, :] = record(kept[source[0]], source[1])

    payload = array(META, LANES)
    return call(body, title, tuple(buffers), (payload, payload))


def thirds(values):
    high = values.astype(jnp.bfloat16)
    rest = values - high.astype(jnp.float32)
    middle = rest.astype(jnp.bfloat16)
    low = (rest - middle.astype(jnp.float32)).astype(jnp.bfloat16)
    return high, middle, low


def pick(hot, values):
    found = None
    for part in thirds(values):
        term = lax.dot_general(
            hot, part, (((1,), (0,)), ((), ())), preferred_element_type=jnp.float32
        )
        found = term if found is None else found + term
    return found


def cell_axes():
    lane = lax.broadcasted_iota(jnp.int32, (TPD, CELLS), 1)
    return lane >> 6, (lane >> 3) & 7, lane & 7


def turn(values, shift):
    return pltpu.roll(values, shift % CELLS, 1)


def beside(values, ghost, facing):
    axis, step = facing // 2, (64, 8, 1)[facing // 2]
    index = cell_axes()[axis]
    if facing % 2 == 0:
        return jnp.where(index == 7, turn(ghost, 7 * step), turn(values, -step))
    return jnp.where(index == 0, turn(ghost, -7 * step), turn(values, step))


def table_of(refs, begin):
    rows = [ref[:, begin : begin + CELLS] for ref in refs]
    return jnp.concatenate(rows + [jnp.zeros((LANES - 7 * TPD, CELLS), jnp.float32)], axis=0)


def ghosts_of(hot, refs):
    found = pick(hot, table_of(refs, 0))
    return [found[TPD * facing : TPD * (facing + 1)] for facing in range(6)]


def gather_grid(arrivals, accs):
    names = ("xp", "xm", "yp", "ym", "zp", "zm")

    def body(*refs):
        kept = dict(zip(names, refs[:6]))
        own = refs[6 : 6 + len(accs)]
        velocity, fluid_out, slots_out, rec = refs[6 + len(accs) :]
        for number, source in enumerate(consumed):
            rec[number * REC : (number + 1) * REC, :] = record(kept[source[0]], source[1])
            slots_out[number : number + 1, :] = slot_row(kept, source, None)
        rec[NBR_BINS * REC : 32 * REC, :] = jnp.zeros(((32 - NBR_BINS) * REC, LANES), jnp.float32)
        slots_out[NBR_BINS:32, :] = jnp.full((32 - NBR_BINS, LANES), -1.0, jnp.float32)
        hot = (
            slots_out[...] == lax.broadcasted_iota(jnp.int32, (32, LANES), 1).astype(jnp.float32)
        ).astype(jnp.float32)
        hot = jnp.transpose(hot)[:TPD, :].astype(jnp.bfloat16)
        received = jnp.concatenate([rec[pl.ds(r, 32, stride=REC), :] for r in range(REC)], axis=1)
        totals = pick(hot, received)
        for acc in own:
            totals = totals + jnp.concatenate(
                [acc[pl.ds(r, TPD, stride=REC), :] for r in range(REC)], axis=1
            )
        masses = totals[:, :CELLS]
        fluid = masses > 0.0
        safe = jnp.where(fluid, masses, 1.0)
        for a in range(3):
            value = totals[:, (a + 1) * CELLS : (a + 2) * CELLS] / safe
            if a == 1:
                value = value - 0.5
            velocity[:, a * CELLS : (a + 1) * CELLS] = jnp.where(fluid, value, 0.0)
        fluid_out[...] = fluid.astype(jnp.float32)

    return call(
        body,
        "gather_grid",
        (*arrivals, *accs),
        (
            array(TPD, 3 * CELLS),
            array(TPD, CELLS),
            array(32, LANES),
        ),
        scratch_shapes=[pltpu.VMEM((32 * REC, LANES), jnp.float32)],
    )


def divergence(arrivals, code_row, code_column, velocity, fluid, arrived):
    def body(*refs):
        payloads, code_row, code_column, fluid = refs[:6], refs[6], refs[7], refs[8]
        fields = refs[9:16]
        hot_out, div_out, pressure = refs[16:]
        group = lax.broadcasted_iota(jnp.int32, (1, LANES), 1) // TPD
        codes = jnp.where(group == 0, code_row[0:1, :], -9999.0)
        for number, ref in enumerate(payloads):
            odd = lax.axis_index(AXES[number // 2]) & 1
            slot = 2 * (number // 2) + 2 - (number + odd) % 2
            codes = jnp.where(group == slot, ref[META + GROUP : META + GROUP + 1, :], codes)
        hots = [
            (code_column[...] + float(step) == codes).astype(jnp.bfloat16) for step in face_codes
        ]
        hot = jnp.concatenate(hots, axis=0)
        hot_out[...] = hot
        total = None
        for a in range(3):
            table = table_of(fields, a * CELLS)
            found = pick(hot[2 * a * TPD : (2 * a + 2) * TPD], table)
            own = fields[0][:, a * CELLS : (a + 1) * CELLS]
            term = 0.5 * (beside(own, found[:TPD], 2 * a) - beside(own, found[TPD:], 2 * a + 1))
            total = term if total is None else total + term
        div_out[...] = total
        pressure[...] = jnp.where(fluid[...] > 0.0, (0.0 - total) / 6.0, 0.0)

    field = array(TPD, CELLS)
    return call(
        body,
        "divergence",
        (*arrivals, code_row, code_column, fluid, velocity, *arrived),
        (array(6 * TPD, LANES, dtype=jnp.bfloat16), field, field),
    )


def sweep(hot, div, fluid, pressure, arrived):
    def body(hot, div, fluid, *refs):
        fields, out = refs[:7], refs[7]
        values = fields[0][...]
        total = None
        for facing, ghost in enumerate(ghosts_of(hot[...], fields)):
            term = beside(values, ghost, facing)
            total = term if total is None else total + term
        out[...] = jnp.where(fluid[...] > 0.0, (total - div[...]) / 6.0, 0.0)

    return call(
        body,
        "sweep",
        (hot, div, fluid, pressure, *arrived),
        array(TPD, CELLS),
    )


def project(hot, fluid, velocity, slots, pressure, arrived):
    def body(hot, fluid, velocity, slots, *refs):
        fields = refs[:7]
        grid_out, tiles, back_p, back_m, back_local, rec = refs[7:]
        values = fields[0][...]
        ghosts = ghosts_of(hot[...], fields)
        wet = fluid[...] > 0.0
        tiles[...] = jnp.zeros_like(tiles)
        rec[...] = jnp.zeros_like(rec)
        named = (
            slots[...] == lax.broadcasted_iota(jnp.int32, (32, LANES), 1).astype(jnp.float32)
        ).astype(jnp.bfloat16)[:, :TPD]
        for a in range(3):
            slope = 0.5 * (
                beside(values, ghosts[2 * a], 2 * a) - beside(values, ghosts[2 * a + 1], 2 * a + 1)
            )
            final = jnp.where(wet, velocity[:, a * CELLS : (a + 1) * CELLS] - slope, 0.0)
            grid_out[a] = final
            copies = pick(named, final)
            for u in range(UPPER):
                row = a * UPPER + u
                tiles[pl.ds(row, TPD, stride=REC), :] = final[:, u * LANES : (u + 1) * LANES]
                rec[pl.ds(row, 32, stride=REC), :] = copies[:, u * LANES : (u + 1) * LANES]
        back_p[...] = rec[:META, :]
        back_m[...] = rec[META : 2 * META, :]
        back_local[...] = rec[2 * META : NBR_BINS * REC, :]

    block = array(META, LANES)
    return call(
        body,
        "project",
        (hot, fluid, velocity, slots, pressure, *arrived),
        (
            array(3, TPD, CELLS),
            array(TPD * REC, LANES),
            block,
            block,
            array(8 * REC, LANES),
        ),
        scratch_shapes=[pltpu.VMEM((32 * REC, LANES), jnp.float32)],
    )


def sample_row(cell, out, tile, row, count):
    upper, hot = upper_and_hot(cell, row, count)
    high = tile.astype(jnp.bfloat16)
    low = (tile - high.astype(jnp.float32)).astype(jnp.bfloat16)
    planes = lax.dot_general(
        jnp.concatenate([high, low], axis=0),
        hot,
        (((1,), (0,)), ((), ())),
        preferred_element_type=jnp.float32,
    )
    planes = planes[:REC] + planes[REC:]
    wanted = (lax.broadcasted_iota(jnp.int32, (8, PPT), 0) & (UPPER - 1)) == upper
    sums = []
    for half in range(2):
        kept = jnp.where(wanted, planes[8 * half : 8 * half + 8], 0.0)
        kept = kept + pltpu.roll(kept, 7, 0)
        sums.append(kept + pltpu.roll(kept, 6, 0))
    out[0, row : row + 1, :] = sums[0][0:1]
    out[1, row : row + 1, :] = sums[0][4:5]
    out[2, row : row + 1, :] = sums[1][0:1]


particle_shape = jax.ShapeDtypeStruct((3, BINS, PPT), jnp.float32)


def sample_own(counts, slots, cell, tiles, sampled, start, blocks):
    def body(counts, slots, cell, tiles, *refs):
        out = refs[-1]
        base = (pl.program_id(0) + start) * 8

        for row in range(8):
            place = pl.multiple_of(slots[base + row] * REC, REC)
            sample_row(cell, out, tiles[pl.ds(place, REC), :], row, counts[base + row])

    args = [counts, slots, cell, near(tiles)]
    specs = [
        scalars(),
        scalars(),
        pl.BlockSpec((8, PPT), lambda i: (i + start, 0)),
        held(),
    ]
    alias = {}
    if sampled is not None:
        args.append(sampled)
        specs.append(pl.BlockSpec(memory_space=pl.ANY))
        alias = {4: 0}
    return call(
        body,
        "sample_own",
        tuple(args),
        particle_shape,
        flops=blocks * 8 * 2_000_000,
        grid=(blocks,),
        in_specs=specs,
        out_specs=pl.BlockSpec((3, 8, PPT), lambda i: (0, i + start, 0)),
        input_output_aliases=alias,
    )


def sample_nbr(counts, cell, buffers, sampled):
    names = ("xp", "xm", "yp", "ym", "zp", "zm")
    first_block = OWN_BINS // 8
    blocks = -(-NBR_BINS // 8)

    def body(counts, cell, *refs):
        kept = dict(zip(names, refs[:6]))
        out, rec = refs[7:]
        step = pl.program_id(0)

        @pl.when(step == 0)
        def _():
            for number, source in enumerate(final_sources):
                rec[number * REC : (number + 1) * REC, :] = record(kept[source[0]], source[1])

        def sample(rows):
            for row in range(rows):
                number = step * 8 + row
                place = pl.multiple_of(number * REC, REC)
                sample_row(cell, out, rec[pl.ds(place, REC), :], row, counts[OWN_BINS + number])

        @pl.when(step < blocks - 1)
        def _():
            sample(8)

        @pl.when(step == blocks - 1)
        def _():
            sample(NBR_BINS - 8 * (blocks - 1))

    return call(
        body,
        "sample_nbr",
        (counts, cell, *[near(buffer) for buffer in buffers], sampled),
        particle_shape,
        flops=NBR_BINS * 2_000_000,
        grid=(blocks,),
        in_specs=[scalars(), pl.BlockSpec((8, PPT), lambda i: (i + first_block, 0))]
        + [held()] * 6
        + [pl.BlockSpec(memory_space=pl.ANY)],
        out_specs=pl.BlockSpec((3, 8, PPT), lambda i: (0, i + first_block, 0)),
        input_output_aliases={8: 0},
        scratch_shapes=[pltpu.VMEM((NBR_BINS * REC, LANES), jnp.float32)],
    )


def exchange(values):
    return [swap(values, axis, which) for axis in AXES for which in (0, 1)]


def together(*values):
    return lax.optimization_barrier(values)


def with_kept(sources):
    return [("kept", n - 18) if name == "rec" else (name, n) for name, n in sources]


def local(tile_coords, owner_map, bin_tile, counts, cell, offset, velocity, affine, mass):
    parts = (
        cell,
        jnp.transpose(offset, (1, 0, 2)),
        jnp.transpose(velocity, (1, 0, 2)),
        jnp.transpose(affine, (1, 0, 2)),
        mass,
    )
    slots, code_row, code_column, slot_rows, below, middle, above = splat_nbr(
        tile_coords, owner_map, bin_tile, counts, parts
    )
    xp, xm = ring(above, "gx", 1), ring(below, "gx", -1)
    acc_x = splat_own(counts, slots, parts, 0, 2)
    xp, xm, acc_x = together(xp, xm, acc_x)
    up, down = forward(
        ("mid", "xp", "xm"),
        (middle, xp, xm),
        slot_rows,
        code_row,
        (y_sources(1), y_sources(-1)),
        "forward_y",
    )
    slots, up, down = together(slots, up, down)
    yp, ym = ring(up, "gy", 1), ring(down, "gy", -1)
    acc_y = splat_own(counts, slots, parts, 2, 1)
    yp, ym, acc_y = together(yp, ym, acc_y)
    up, down = forward(
        ("mid", "xp", "xm", "yp", "ym"),
        (middle, xp, xm, yp, ym),
        slot_rows,
        code_row,
        (z_sources(1), z_sources(-1)),
        "forward_z",
    )
    slots, up, down = together(slots, up, down)
    zp, zm = ring(up, "gz", 1), ring(down, "gz", -1)
    acc_z = splat_own(counts, slots, parts, 3, 1)
    arrivals = (xp, xm, yp, ym, zp, zm)
    grid_u, fluid, nbr_slots = gather_grid(arrivals, (acc_x, acc_y, acc_z))
    hot, div, pressure = divergence(
        arrivals, code_row, code_column, grid_u, fluid, exchange(grid_u)
    )
    for _ in range(SWEEPS - 1):
        pressure = sweep(hot, div, fluid, pressure, exchange(pressure))
    grid_v, tiles, back_p, back_m, kept = project(
        hot, fluid, grid_u, nbr_slots, pressure, exchange(pressure)
    )
    rzp, rzm = ring(back_p, "gz", -1), ring(back_m, "gz", 1)
    sampled = sample_own(counts, slots, cell, tiles, None, 0, 2)
    rzp, rzm, sampled = together(rzp, rzm, sampled)
    up, down = reply(
        ("kept", "zp", "zm"),
        (kept, rzp, rzm),
        (with_kept(y_reply_sources(1)), with_kept(y_reply_sources(-1))),
        "reply_y",
    )
    slots, up, down = together(slots, up, down)
    ryp, rym = ring(up, "gy", -1), ring(down, "gy", 1)
    sampled = sample_own(counts, slots, cell, tiles, sampled, 2, 1)
    ryp, rym, sampled = together(ryp, rym, sampled)
    up, down = reply(
        ("kept", "zp", "zm", "yp", "ym"),
        (kept, rzp, rzm, ryp, rym),
        (with_kept(x_reply_sources(1)), with_kept(x_reply_sources(-1))),
        "reply_x",
    )
    slots, up, down = together(slots, up, down)
    rxp, rxm = ring(up, "gx", -1), ring(down, "gx", 1)
    sampled = sample_own(counts, slots, cell, tiles, sampled, 3, 1)
    sampled = sample_nbr(counts, cell, (rxp, rxm, ryp, rym, rzp, rzm), sampled)
    return (
        grid_v.reshape(3, TPD * CELLS),
        pressure.reshape(-1),
        jnp.transpose(sampled, (1, 0, 2)),
    )


def solution(mesh):
    split = P(AXES)
    particles = P(AXES, None, None)
    return jax.shard_map(
        local,
        mesh=mesh,
        in_specs=(
            P(None, AXES),
            P(),
            split,
            split,
            P(AXES, None),
            particles,
            particles,
            particles,
            P(AXES, None),
        ),
        out_specs=(P(None, AXES), split, particles),
        check_vma=False,
    )
```

time: 557 us -> 108 us (0.19)
  the two profiles are of different devices: /device:TPU:116 before, /device:TPU:1 now
where the time goes in v1:
time: 108 us; the launch traced here: 107 us
  starting transfers between devices  50.2 us (46%)
  Pallas kernels  34.8 us (32%)
  waiting for transfers between devices  19.9 us (18%)
  local copies, waits for them, and re-layouts  1.35 us (1%)
    pallas_call x18, Pallas kernels, call(): pl.pallas_call(body, out_shape=outs, name=name, cost_estimate=pl.CostEsti...  34.8 us
    ppermute x30, starting transfers between devices, swap(): return lax.ppermute(block, axis, [(i, j % size) for i, j in pairs])  33.4 us
    ppermute x12, starting transfers between devices, ring(): lax.ppermute(block, axis, [(i, (i + distance) % size) for i in range(size)])  16.9 us
    ppermute x30, waiting for transfers between devices, swap(): return lax.ppermute(block, axis, [(i, j % size) for i, j in pairs])  16.5 us
    ppermute x12, waiting for transfers between devices, ring(): lax.ppermute(block, axis, [(i, (i + distance) % size) for i in range(size)])  3.37 us
  transfers between devices with their start and end apart: 42, of which 12 were waited for; matrix products, arithmetic and copies ran while one was open for 1% of the time, Pallas kernels for 18%

profile of v1, /device:TPU:1, one launch (start us, length us, event | category | flops | bytes accessed | tf_op | source)
XLA Modules:
  0.0 107.2 jit_solution(3608969920909701410)
XLA Ops:
  0.6 6.5 %splat_nbr.1 = (s32[58]{0:T(128)}, f32[8,128]{1,0:T(8,128)S(1)}, f32[16,128]{1,0:T(8,128)S(1)}, f32[32,128]{1,0:T(8,128)S(1)}, f32[160,128]{1,0:T(8,128)S(1)}, /...) custom-call(s32[3,16]{1,0:T(4,128)} %coords.1, s32[4096]{0:T(1024)} %owners.1, s32[58]{0:T(128)} %bin_tile.1, s32[58]{0:T(128)} %counts.15, ...), custom_call_target="tpu_custom_call" | custom-call | flops 52000000 | bytes 500000 | tf_op jit(solution)/shard_map/splat_nbr/pallas_call | solution.py:57
  7.1 2.1 %collective-permute-start = (f32[160,128]{1,0:T(8,128)S(1)}, f32[160,128]{1,0:T(8,128)S(1)}, u32[]{:S(2)}, u32[]{:S(2)}) collective-permute-start(f32[160,128]{1,0:T(8,128)S(1)} %get-tuple-element.53), channel_id=1, source_target_pairs={{0,64},{64,128},{128,192},{192,0},{1,65},{65,129},{129,193},{193,1... | collective-permute-start | bytes 245768 | tf_op jit(solution)/shard_map/ppermute | solution.py:27
  10.6 3.8 %splat_own.3.refs_6_ = f32[256,128]{1,0:T(8,128)S(1)} custom-call(s32[58]{0:T(128)} %counts.15, s32[58]{0:T(128)} %get-tuple-element.101.slots, s32[58,2048]{1,0:T(8,128)} %cell.15, f32[3,58,2048]{2,1,0:T(8,128)} %bitcast.15, f32[3,58,2048]{2,1,0:T(8,128)} %bitcast.19, f32[9,58,2048]{2,1,0:T(8,128)} %bitcast.11, f32[58,2048]{1,0:T(8,128)} %mass.7), custom_call_target="tpu_custom_call" | custom-call | flops 32000000 | bytes 500000 | tf_op jit(solution)/shard_map/splat_own/pallas_call | solution.py:57
  16.3 4.0 %collective-permute-start.3 = (f32[160,128]{1,0:T(8,128)S(1)}, f32[160,128]{1,0:T(8,128)S(1)}, u32[]{:S(2)}, u32[]{:S(2)}) collective-permute-start(f32[160,128]{1,0:T(8,128)S(1)} %get-tuple-element.64), channel_id=1, source_target_pairs={{0,56},{8,0},{16,8},{24,16},{32,24},{40,32},{48,40},{56,48},{1,57}... | collective-permute-start | bytes 245768 | tf_op jit(solution)/shard_map/ppermute | solution.py:27
  20.3 2.5 %splat_own.4.refs_7_ = f32[256,128]{1,0:T(8,128)S(1)} custom-call(s32[58]{0:T(128)} %counts.15, s32[58]{0:T(128)} %get-tuple-element.101.slots, s32[58,2048]{1,0:T(8,128)} %cell.15, f32[3,58,2048]{2,1,0:T(8,128)} %bitcast.16, f32[3,58,2048]{2,1,0:T(8,128)} %bitcast.20, f32[9,58,2048]{2,1,0:T(8,128)} %bitcast.12, f32[58,2048]{1,0:T(8,128)} %mass.7), custom_call_target="tpu_custom_call" | custom-call | flops 16000000 | bytes 500000 | tf_op jit(solution)/shard_map/splat_own/pallas_call | solution.py:57
  22.8 2.7 %collective-permute-start.4 = (f32[160,128]{1,0:T(8,128)S(1)}, f32[160,128]{1,0:T(8,128)S(1)}, u32[]{:S(2)}, u32[]{:S(2)}) collective-permute-start(f32[160,128]{1,0:T(8,128)S(1)} %get-tuple-element.70), channel_id=1, source_target_pairs={{0,1},{1,2},{2,3},{3,4},{4,5},{5,6},{6,7},{7,0},{8,9},{9,10},{10,1... | collective-permute-start | bytes 245768 | tf_op jit(solution)/shard_map/ppermute | solution.py:27
  25.6 2.5 %splat_own.5.refs_8_ = f32[256,128]{1,0:T(8,128)S(1)} custom-call(s32[58]{0:T(128)} %counts.15, s32[58]{0:T(128)} %get-tuple-element.101.slots, s32[58,2048]{1,0:T(8,128)} %cell.15, f32[3,58,2048]{2,1,0:T(8,128)} %bitcast.17, f32[3,58,2048]{2,1,0:T(8,128)} %bitcast.21, f32[9,58,2048]{2,1,0:T(8,128)} %bitcast.13, f32[58,2048]{1,0:T(8,128)} %mass.7), custom_call_target="tpu_custom_call" | custom-call | flops 16000000 | bytes 500000 | tf_op jit(solution)/shard_map/splat_own/pallas_call | solution.py:57
  33.4 3.3 %collective-permute-start.9 = (f32[16,1536]{1,0:T(8,128)S(1)}, f32[16,1536]{1,0:T(8,128)S(1)}, u32[]{:S(2)}, u32[]{:S(2)}) collective-permute-start(f32[16,1536]{1,0:T(8,128)S(1)} %get-tuple-element.77.refs_9_.velocity), channel_id=1, source_target_pairs={{0,56},{8,16},{16,8},{24,32},{32,24},{40,48},{48,40},{56,0},{1,57}... | collective-permute-start | bytes 294920 | tf_op jit(solution)/shard_map/ppermute | solution.py:33
  40.9 1.9 %collective-permute-start.14 = (f32[16,512]{1,0:T(8,128)S(1)}, f32[16,512]{1,0:T(8,128)S(1)}, u32[]{:S(2)}, u32[]{:S(2)}) collective-permute-start(f32[16,512]{1,0:T(8,128)S(1)} %get-tuple-element.81.refs_0_), channel_id=1, source_target_pairs={{0,8},{8,0},{16,24},{24,16},{32,40},{40,32},{48,56},{56,48},{1,9},... | collective-permute-start | bytes 98312 | tf_op jit(solution)/shard_map/ppermute | solution.py:33
  43.6 4.2 %collective-permute-start.16 = (f32[16,512]{1,0:T(8,128)S(1)}, f32[16,512]{1,0:T(8,128)S(1)}, u32[]{:S(2)}, u32[]{:S(2)}) collective-permute-start(f32[16,512]{1,0:T(8,128)S(1)} %get-tuple-element.81.refs_0_), channel_id=1, source_target_pairs={{0,1},{1,0},{2,3},{3,2},{4,5},{5,4},{6,7},{7,6},{8,9},{9,8},{10,11... | collective-permute-start | bytes 98312 | tf_op jit(solution)/shard_map/ppermute | solution.py:33
  48.7 2.8 %collective-permute-done.17.refs_6_ = f32[16,512]{1,0:T(8,128)S(1)} collective-permute-done((f32[16,512]{1,0:T(8,128)S(1)}, f32[16,512]{1,0:T(8,128)S(1)}, u32[]{:S(2)}, u32[]{:S(2)}) %collective-permute-start.17) | collective-permute-done | bytes 32800 | tf_op jit(solution)/shard_map/ppermute | solution.py:33
  53.8 1.8 %collective-permute-start.20 = (f32[16,512]{1,0:T(8,128)S(1)}, f32[16,512]{1,0:T(8,128)S(1)}, u32[]{:S(2)}, u32[]{:S(2)}) collective-permute-start(f32[16,512]{1,0:T(8,128)S(1)} %sweep.3.refs_0_), channel_id=1, source_target_pairs={{0,8},{8,0},{16,24},{24,16},{32,40},{40,32},{48,56},{56,48},{1,9},... | collective-permute-start | bytes 98312 | tf_op jit(solution)/shard_map/ppermute | solution.py:33
  56.1 2.0 %collective-permute-start.22 = (f32[16,512]{1,0:T(8,128)S(1)}, f32[16,512]{1,0:T(8,128)S(1)}, u32[]{:S(2)}, u32[]{:S(2)}) collective-permute-start(f32[16,512]{1,0:T(8,128)S(1)} %sweep.3.refs_0_), channel_id=1, source_target_pairs={{0,1},{1,0},{2,3},{3,2},{4,5},{5,4},{6,7},{7,6},{8,9},{9,8},{10,11... | collective-permute-start | bytes 98312 | tf_op jit(solution)/shard_map/ppermute | solution.py:33
  59.6 2.2 %collective-permute-done.23.refs_6_ = f32[16,512]{1,0:T(8,128)S(1)} collective-permute-done((f32[16,512]{1,0:T(8,128)S(1)}, f32[16,512]{1,0:T(8,128)S(1)}, u32[]{:S(2)}, u32[]{:S(2)}) %collective-permute-start.23) | collective-permute-done | bytes 32800 | tf_op jit(solution)/shard_map/ppermute | solution.py:33
  64.5 2.2 %collective-permute-start.27 = (f32[16,512]{1,0:T(8,128)S(1)}, f32[16,512]{1,0:T(8,128)S(1)}, u32[]{:S(2)}, u32[]{:S(2)}) collective-permute-start(f32[16,512]{1,0:T(8,128)S(1)} %sweep.4.refs_0_), channel_id=1, source_target_pairs={{0,56},{8,16},{16,8},{24,32},{32,24},{40,48},{48,40},{56,0},{1,57}... | collective-permute-start | bytes 98312 | tf_op jit(solution)/shard_map/ppermute | solution.py:33
  66.7 2.0 %collective-permute-start.28 = (f32[16,512]{1,0:T(8,128)S(1)}, f32[16,512]{1,0:T(8,128)S(1)}, u32[]{:S(2)}, u32[]{:S(2)}) collective-permute-start(f32[16,512]{1,0:T(8,128)S(1)} %sweep.4.refs_0_), channel_id=1, source_target_pairs={{0,1},{1,0},{2,3},{3,2},{4,5},{5,4},{6,7},{7,6},{8,9},{9,8},{10,11... | collective-permute-start | bytes 98312 | tf_op jit(solution)/shard_map/ppermute | solution.py:33
  69.6 2.8 %collective-permute-done.29.refs_6_ = f32[16,512]{1,0:T(8,128)S(1)} collective-permute-done((f32[16,512]{1,0:T(8,128)S(1)}, f32[16,512]{1,0:T(8,128)S(1)}, u32[]{:S(2)}, u32[]{:S(2)}) %collective-permute-start.29) | collective-permute-done | bytes 32800 | tf_op jit(solution)/shard_map/ppermute | solution.py:33
  75.6 2.0 %collective-permute-start.34 = (f32[16,512]{1,0:T(8,128)S(1)}, f32[16,512]{1,0:T(8,128)S(1)}, u32[]{:S(2)}, u32[]{:S(2)}) collective-permute-start(f32[16,512]{1,0:T(8,128)S(1)} %sweep.5.refs_0_), channel_id=1, source_target_pairs={{0,1},{1,0},{2,3},{3,2},{4,5},{5,4},{6,7},{7,6},{8,9},{9,8},{10,11... | collective-permute-start | bytes 98312 | tf_op jit(solution)/shard_map/ppermute | solution.py:33
  78.8 2.5 %collective-permute-done.35.refs_6_ = f32[16,512]{1,0:T(8,128)S(1)} collective-permute-done((f32[16,512]{1,0:T(8,128)S(1)}, f32[16,512]{1,0:T(8,128)S(1)}, u32[]{:S(2)}, u32[]{:S(2)}) %collective-permute-start.35) | collective-permute-done | bytes 32800 | tf_op jit(solution)/shard_map/ppermute | solution.py:33
  83.6 4.6 %sample_own.3.refs_0_ = f32[3,58,2048]{2,1,0:T(8,128)} custom-call(s32[58]{0:T(128)} %counts.15, s32[58]{0:T(128)} %get-tuple-element.101.slots, s32[58,2048]{1,0:T(8,128)} %cell.15, f32[256,128]{1,0:T(8,128)S(1)} %get-tuple-element.86.tiles), custom_call_target="tpu_custom_call" | custom-call | flops 32000000 | bytes 500000 | tf_op jit(solution)/shard_map/sample_own/pallas_call | solution.py:57
  89.7 3.0 %sample_own.4.refs_0_ = f32[3,58,2048]{2,1,0:T(8,128)} custom-call(s32[58]{0:T(128)} %counts.15, s32[58]{0:T(128)} %get-tuple-element.101.slots, s32[58,2048]{1,0:T(8,128)} %cell.15, f32[256,128]{1,0:T(8,128)S(1)} %get-tuple-element.86.tiles, f32[3,58,2048]{2,1,0:T(8,128)} %sample_own.3.refs_0_), custom_call_target="tpu_custom_call", output_to_operand_aliasing={{}: (4, {})} | custom-call | flops 16000000 | bytes 500000 | tf_op jit(solution)/shard_map/sample_own/pallas_call | solution.py:57
  92.8 2.0 %collective-permute-done.39.refs_4_.refs_3_ = f32[144,128]{1,0:T(8,128)S(1)} collective-permute-done((f32[144,128]{1,0:T(8,128)S(1)}, f32[144,128]{1,0:T(8,128)S(1)}, u32[]{:S(2)}, u32[]{:S(2)}) %collective-permute-start.39) | collective-permute-done | bytes 73760 | tf_op jit(solution)/shard_map/ppermute | solution.py:27
  97.6 3.0 %sample_own.5.refs_6_ = f32[3,58,2048]{2,1,0:T(8,128)} custom-call(s32[58]{0:T(128)} %counts.15, s32[58]{0:T(128)} %get-tuple-element.101.slots, s32[58,2048]{1,0:T(8,128)} %cell.15, f32[256,128]{1,0:T(8,128)S(1)} %get-tuple-element.86.tiles, f32[3,58,2048]{2,1,0:T(8,128)} %sample_own.4.refs_0_), custom_call_target="tpu_custom_call", output_to_operand_aliasing={{}: (4, {})} | custom-call | flops 16000000 | bytes 500000 | tf_op jit(solution)/shard_map/sample_own/pallas_call | solution.py:57
  100.7 6.5 %sample_nbr.1 = f32[3,58,2048]{2,1,0:T(8,128)} custom-call(s32[58]{0:T(128)} %counts.15, s32[58,2048]{1,0:T(8,128)} %cell.15, f32[144,128]{1,0:T(8,128)S(1)} %collective-permute-done.40.refs_0_, f32[144,128]{1,0:T(8,128)S(1)} %collective-permute-done.41.refs_1_, ...), custom_call_target="tpu_custom_call", output_to_operand_aliasing={{}: (8, {})} | custom-call | flops 52000000 | bytes 500000 | tf_op jit(solution)/shard_map/sample_nbr/pallas_call | solution.py:57
  (80 shorter events, 33.3 us)
Async XLA Ops:
  7.1 7.3 %collective-permute-start = (f32[160,128]{1,0:T(8,128)S(1)}, f32[160,128]{1,0:T(8,128)S(1)}, u32[]{:S(2)}, u32[]{:S(2)}) collective-permute-start(f32[160,128]{1,0:T(8,128)S(1)} %get-tuple-element.53), channel_id=1, source_target_pairs={{0,64},{64,128},{128,192},{192,0},{1,65},{65,129},{129,193},{193,1... | collective-permute-start | bytes 245768 | tf_op jit(solution)/shard_map/ppermute | solution.py:27
  9.2 5.2 %collective-permute-start.1 = (f32[160,128]{1,0:T(8,128)S(1)}, f32[160,128]{1,0:T(8,128)S(1)}, u32[]{:S(2)}, u32[]{:S(2)}) collective-permute-start(f32[160,128]{1,0:T(8,128)S(1)} %get-tuple-element.54), channel_id=1, source_target_pairs={{0,192},{64,0},{128,64},{192,128},{1,193},{65,1},{129,65},{193,129... | collective-permute-start | bytes 245768 | tf_op jit(solution)/shard_map/ppermute | solution.py:27
  14.4 8.4 %collective-permute-start.2 = (f32[160,128]{1,0:T(8,128)S(1)}, f32[160,128]{1,0:T(8,128)S(1)}, u32[]{:S(2)}, u32[]{:S(2)}) collective-permute-start(f32[160,128]{1,0:T(8,128)S(1)} %get-tuple-element.63), channel_id=1, source_target_pairs={{0,8},{8,16},{16,24},{24,32},{32,40},{40,48},{48,56},{56,0},{1,9},... | collective-permute-start | bytes 245768 | tf_op jit(solution)/shard_map/ppermute | solution.py:27
  16.3 6.6 %collective-permute-start.3 = (f32[160,128]{1,0:T(8,128)S(1)}, f32[160,128]{1,0:T(8,128)S(1)}, u32[]{:S(2)}, u32[]{:S(2)}) collective-permute-start(f32[160,128]{1,0:T(8,128)S(1)} %get-tuple-element.64), channel_id=1, source_target_pairs={{0,56},{8,0},{16,8},{24,16},{32,24},{40,32},{48,40},{56,48},{1,57}... | collective-permute-start | bytes 245768 | tf_op jit(solution)/shard_map/ppermute | solution.py:27
  22.8 5.2 %collective-permute-start.4 = (f32[160,128]{1,0:T(8,128)S(1)}, f32[160,128]{1,0:T(8,128)S(1)}, u32[]{:S(2)}, u32[]{:S(2)}) collective-permute-start(f32[160,128]{1,0:T(8,128)S(1)} %get-tuple-element.70), channel_id=1, source_target_pairs={{0,1},{1,2},{2,3},{3,4},{4,5},{5,6},{6,7},{7,0},{8,9},{9,10},{10,1... | collective-permute-start | bytes 245768 | tf_op jit(solution)/shard_map/ppermute | solution.py:27
  30.3 6.3 %collective-permute-start.11 = (f32[16,1536]{1,0:T(8,128)S(1)}, f32[16,1536]{1,0:T(8,128)S(1)}, u32[]{:S(2)}, u32[]{:S(2)}) collective-permute-start(f32[16,1536]{1,0:T(8,128)S(1)} %get-tuple-element.77.refs_9_.velocity), channel_id=1, source_target_pairs={{0,7},{1,2},{2,1},{3,4},{4,3},{5,6},{6,5},{7,0},{8,15},{9,10},{10,... | collective-permute-start | bytes 294920 | tf_op jit(solution)/shard_map/ppermute | solution.py:33
  31.5 5.1 %collective-permute-start.6 = (f32[16,1536]{1,0:T(8,128)S(1)}, f32[16,1536]{1,0:T(8,128)S(1)}, u32[]{:S(2)}, u32[]{:S(2)}) collective-permute-start(f32[16,1536]{1,0:T(8,128)S(1)} %get-tuple-element.77.refs_9_.velocity), channel_id=1, source_target_pairs={{0,64},{64,0},{128,192},{192,128},{1,65},{65,1},{129,193},{193,129... | collective-permute-start | bytes 294920 | tf_op jit(solution)/shard_map/ppermute | solution.py:33
  31.6 5.0 %collective-permute-start.7 = (f32[16,1536]{1,0:T(8,128)S(1)}, f32[16,1536]{1,0:T(8,128)S(1)}, u32[]{:S(2)}, u32[]{:S(2)}) collective-permute-start(f32[16,1536]{1,0:T(8,128)S(1)} %get-tuple-element.77.refs_9_.velocity), channel_id=1, source_target_pairs={{0,192},{64,128},{128,64},{192,0},{1,193},{65,129},{129,65},{193,1... | collective-permute-start | bytes 294920 | tf_op jit(solution)/shard_map/ppermute | solution.py:33
  33.4 5.3 %collective-permute-start.9 = (f32[16,1536]{1,0:T(8,128)S(1)}, f32[16,1536]{1,0:T(8,128)S(1)}, u32[]{:S(2)}, u32[]{:S(2)}) collective-permute-start(f32[16,1536]{1,0:T(8,128)S(1)} %get-tuple-element.77.refs_9_.velocity), channel_id=1, source_target_pairs={{0,56},{8,16},{16,8},{24,32},{32,24},{40,48},{48,40},{56,0},{1,57}... | collective-permute-start | bytes 294920 | tf_op jit(solution)/shard_map/ppermute | solution.py:33
  39.1 8.7 %collective-permute-start.12 = (f32[16,512]{1,0:T(8,128)S(1)}, f32[16,512]{1,0:T(8,128)S(1)}, u32[]{:S(2)}, u32[]{:S(2)}) collective-permute-start(f32[16,512]{1,0:T(8,128)S(1)} %get-tuple-element.81.refs_0_), channel_id=1, source_target_pairs={{0,64},{64,0},{128,192},{192,128},{1,65},{65,1},{129,193},{193,129... | collective-permute-start | bytes 98312 | tf_op jit(solution)/shard_map/ppermute | solution.py:33
  39.7 8.2 %collective-permute-start.13 = (f32[16,512]{1,0:T(8,128)S(1)}, f32[16,512]{1,0:T(8,128)S(1)}, u32[]{:S(2)}, u32[]{:S(2)}) collective-permute-start(f32[16,512]{1,0:T(8,128)S(1)} %get-tuple-element.81.refs_0_), channel_id=1, source_target_pairs={{0,192},{64,128},{128,64},{192,0},{1,193},{65,129},{129,65},{193,1... | collective-permute-start | bytes 98312 | tf_op jit(solution)/shard_map/ppermute | solution.py:33
  40.9 7.0 %collective-permute-start.14 = (f32[16,512]{1,0:T(8,128)S(1)}, f32[16,512]{1,0:T(8,128)S(1)}, u32[]{:S(2)}, u32[]{:S(2)}) collective-permute-start(f32[16,512]{1,0:T(8,128)S(1)} %get-tuple-element.81.refs_0_), channel_id=1, source_target_pairs={{0,8},{8,0},{16,24},{24,16},{32,40},{40,32},{48,56},{56,48},{1,9},... | collective-permute-start | bytes 98312 | tf_op jit(solution)/shard_map/ppermute | solution.py:33
  42.8 5.1 %collective-permute-start.15 = (f32[16,512]{1,0:T(8,128)S(1)}, f32[16,512]{1,0:T(8,128)S(1)}, u32[]{:S(2)}, u32[]{:S(2)}) collective-permute-start(f32[16,512]{1,0:T(8,128)S(1)} %get-tuple-element.81.refs_0_), channel_id=1, source_target_pairs={{0,56},{8,16},{16,8},{24,32},{32,24},{40,48},{48,40},{56,0},{1,57}... | collective-permute-start | bytes 98312 | tf_op jit(solution)/shard_map/ppermute | solution.py:33
  43.6 5.1 %collective-permute-start.16 = (f32[16,512]{1,0:T(8,128)S(1)}, f32[16,512]{1,0:T(8,128)S(1)}, u32[]{:S(2)}, u32[]{:S(2)}) collective-permute-start(f32[16,512]{1,0:T(8,128)S(1)} %get-tuple-element.81.refs_0_), channel_id=1, source_target_pairs={{0,1},{1,0},{2,3},{3,2},{4,5},{5,4},{6,7},{7,6},{8,9},{9,8},{10,11... | collective-permute-start | bytes 98312 | tf_op jit(solution)/shard_map/ppermute | solution.py:33
  51.9 6.3 %collective-permute-start.18 = (f32[16,512]{1,0:T(8,128)S(1)}, f32[16,512]{1,0:T(8,128)S(1)}, u32[]{:S(2)}, u32[]{:S(2)}) collective-permute-start(f32[16,512]{1,0:T(8,128)S(1)} %sweep.3.refs_0_), channel_id=1, source_target_pairs={{0,64},{64,0},{128,192},{192,128},{1,65},{65,1},{129,193},{193,129... | collective-permute-start | bytes 98312 | tf_op jit(solution)/shard_map/ppermute | solution.py:33
  52.0 6.2 %collective-permute-start.19 = (f32[16,512]{1,0:T(8,128)S(1)}, f32[16,512]{1,0:T(8,128)S(1)}, u32[]{:S(2)}, u32[]{:S(2)}) collective-permute-start(f32[16,512]{1,0:T(8,128)S(1)} %sweep.3.refs_0_), channel_id=1, source_target_pairs={{0,192},{64,128},{128,64},{192,0},{1,193},{65,129},{129,65},{193,1... | collective-permute-start | bytes 98312 | tf_op jit(solution)/shard_map/ppermute | solution.py:33
  62.2 6.5 %collective-permute-start.24 = (f32[16,512]{1,0:T(8,128)S(1)}, f32[16,512]{1,0:T(8,128)S(1)}, u32[]{:S(2)}, u32[]{:S(2)}) collective-permute-start(f32[16,512]{1,0:T(8,128)S(1)} %sweep.4.refs_0_), channel_id=1, source_target_pairs={{0,64},{64,0},{128,192},{192,128},{1,65},{65,1},{129,193},{193,129... | collective-permute-start | bytes 98312 | tf_op jit(solution)/shard_map/ppermute | solution.py:33
  62.8 5.9 %collective-permute-start.25 = (f32[16,512]{1,0:T(8,128)S(1)}, f32[16,512]{1,0:T(8,128)S(1)}, u32[]{:S(2)}, u32[]{:S(2)}) collective-permute-start(f32[16,512]{1,0:T(8,128)S(1)} %sweep.4.refs_0_), channel_id=1, source_target_pairs={{0,192},{64,128},{128,64},{192,0},{1,193},{65,129},{129,65},{193,1... | collective-permute-start | bytes 98312 | tf_op jit(solution)/shard_map/ppermute | solution.py:33
  72.7 4.9 %collective-permute-start.30 = (f32[16,512]{1,0:T(8,128)S(1)}, f32[16,512]{1,0:T(8,128)S(1)}, u32[]{:S(2)}, u32[]{:S(2)}) collective-permute-start(f32[16,512]{1,0:T(8,128)S(1)} %sweep.5.refs_0_), channel_id=1, source_target_pairs={{0,64},{64,0},{128,192},{192,128},{1,65},{65,1},{129,193},{193,129... | collective-permute-start | bytes 98312 | tf_op jit(solution)/shard_map/ppermute | solution.py:33
  81.8 6.3 %collective-permute-start.36 = (f32[144,128]{1,0:T(8,128)S(1)}, f32[144,128]{1,0:T(8,128)S(1)}, u32[]{:S(2)}, u32[]{:S(2)}) collective-permute-start(f32[144,128]{1,0:T(8,128)S(1)} %get-tuple-element.84), channel_id=1, source_target_pairs={{0,7},{1,0},{2,1},{3,2},{4,3},{5,4},{6,5},{7,6},{8,15},{9,8},{10,9... | collective-permute-start | bytes 221192 | tf_op jit(solution)/shard_map/ppermute | solution.py:27
  82.7 5.4 %collective-permute-start.37 = (f32[144,128]{1,0:T(8,128)S(1)}, f32[144,128]{1,0:T(8,128)S(1)}, u32[]{:S(2)}, u32[]{:S(2)}) collective-permute-start(f32[144,128]{1,0:T(8,128)S(1)} %get-tuple-element.85), channel_id=1, source_target_pairs={{0,1},{1,2},{2,3},{3,4},{4,5},{5,6},{6,7},{7,0},{8,9},{9,10},{10,1... | collective-permute-start | bytes 221192 | tf_op jit(solution)/shard_map/ppermute | solution.py:27
  89.7 5.1 %collective-permute-start.39 = (f32[144,128]{1,0:T(8,128)S(1)}, f32[144,128]{1,0:T(8,128)S(1)}, u32[]{:S(2)}, u32[]{:S(2)}) collective-permute-start(f32[144,128]{1,0:T(8,128)S(1)} %get-tuple-element.93), channel_id=1, source_target_pairs={{0,8},{8,16},{16,24},{24,32},{32,40},{40,48},{48,56},{56,0},{1,9},... | collective-permute-start | bytes 221192 | tf_op jit(solution)/shard_map/ppermute | solution.py:27
  94.7 5.9 %collective-permute-start.40 = (f32[144,128]{1,0:T(8,128)S(1)}, f32[144,128]{1,0:T(8,128)S(1)}, u32[]{:S(2)}, u32[]{:S(2)}) collective-permute-start(f32[144,128]{1,0:T(8,128)S(1)} %get-tuple-element.99), channel_id=1, source_target_pairs={{0,192},{64,0},{128,64},{192,128},{1,193},{65,1},{129,65},{193,129... | collective-permute-start | bytes 221192 | tf_op jit(solution)/shard_map/ppermute | solution.py:27
  95.7 4.9 %collective-permute-start.41 = (f32[144,128]{1,0:T(8,128)S(1)}, f32[144,128]{1,0:T(8,128)S(1)}, u32[]{:S(2)}, u32[]{:S(2)}) collective-permute-start(f32[144,128]{1,0:T(8,128)S(1)} %get-tuple-element.100), channel_id=1, source_target_pairs={{0,64},{64,128},{128,192},{192,0},{1,65},{65,129},{129,193},{193,1... | collective-permute-start | bytes 221192 | tf_op jit(solution)/shard_map/ppermute | solution.py:27
  (18 other events, 69.3 us)

commit v2 on v1

--- a/solution.py
+++ b/solution.py
@@ -63,13 +63,15 @@
     )(*args)
 
 
-def upper_and_hot(cell_ref, row, count):
-    cells = cell_ref[row : row + 1, :]
+def one_hot(cells, width):
+    lower = (cells & (width - 1)).astype(jnp.float32).astype(jnp.bfloat16)
+    index = lax.broadcasted_iota(jnp.int32, (width, PPT), 0).astype(jnp.float32)
+    return jnp.where(index.astype(jnp.bfloat16) == lower, jnp.bfloat16(1), jnp.bfloat16(0))
+
+
+def upper_index(cells, width, count):
     living = lax.broadcasted_iota(jnp.int32, (1, PPT), 1) < count
-    upper = jnp.where(living, cells >> 7, -1)
-    lower = cells & (LANES - 1)
-    hot = (lax.broadcasted_iota(jnp.int32, (LANES, PPT), 0) == lower).astype(jnp.bfloat16)
-    return upper, hot
+    return jnp.where(living, cells >> (width.bit_length() - 1), -1)
 
 
 def store_deposits(off, vel, aff, mass, amounts):
@@ -81,19 +83,29 @@
 
 
 def splat_row(cell, amounts, row, count):
-    upper, hot = upper_and_hot(cell, row, count)
+    half = LANES // 2
+    cells = cell[row : row + 1, :]
+    upper = upper_index(cells, half, count)
     position = lax.broadcasted_iota(jnp.int32, (8, PPT), 0)
-    first = position == upper
-    second = position == jnp.where(upper < 0, -1, upper + UPPER)
-    halves = []
-    for pair in range(2):
-        one = amounts[2 * pair, row : row + 1, :]
-        two = amounts[2 * pair + 1, row : row + 1, :]
-        halves.append(jnp.where(first, one, jnp.where(second, two, 0.0)))
-    weighted = jnp.concatenate(halves, axis=0).astype(jnp.bfloat16)
-    return lax.dot_general(
-        weighted, hot, (((1,), (1,)), ((), ())), preferred_element_type=jnp.float32
-    )
+    chosen = [
+        jnp.where(
+            position < UPPER,
+            amounts[2 * pair, row : row + 1, :],
+            amounts[2 * pair + 1, row : row + 1, :],
+        )
+        for pair in range(2)
+    ]
+    weighted = []
+    for side in range(2):
+        there = 2 * (position & (UPPER - 1)) + side == upper
+        weighted += [jnp.where(there, values, 0.0) for values in chosen]
+    summed = lax.dot_general(
+        jnp.concatenate(weighted, axis=0).astype(jnp.bfloat16),
+        one_hot(cells, half),
+        (((1,), (1,)), ((), ())),
+        preferred_element_type=jnp.float32,
+    )
+    return jnp.concatenate([summed[:REC], summed[REC:]], axis=1)
 
 
 def particle_specs(start):
@@ -132,13 +144,18 @@
     )
 
 
-def splat_nbr(tile_coords, owner_map, bin_tile, counts, parts):
-    first_block = OWN_BINS // 8
-    blocks = -(-NBR_BINS // 8)
-    last = NBR_BINS - 8 * (blocks - 1)
-
+FIRST = OWN_BINS // 8
+side_rows = (tuple(range(8)), (0,), tuple(range(1, 8)), (0, 1))
+middle_rows = {1: tuple(range(1, 8)), 2: (0,)}
+
+
+def side_place(number):
+    return (0, number) if number < GROUP else (1, number - 17)
+
+
+def splat_sides(tile_coords, owner_map, bin_tile, counts, parts):
     def body(coords, owners, bin_tile, counts, cell, off, vel, aff, mass, *rest):
-        slots, code_row, code_column, slot_rows, below, middle, above, rec, amounts = rest
+        slots, code_row, code_column, slot_rows, below, above, amounts = rest
         step = pl.program_id(0)
 
         @pl.when(step == 0)
@@ -157,51 +174,74 @@
                 down = jnp.where(row_of == t, code, down)
             code_row[...] = along.astype(jnp.float32)
             code_column[...] = down.astype(jnp.float32)
-
-        store_deposits(off, vel, aff, mass, amounts)
-
-        def splat(rows):
-            for row in range(rows):
-                number = step * 8 + row
-                rec[pl.ds(pl.multiple_of(number * REC, REC), REC), :] = splat_row(
-                    cell, amounts, row, counts[OWN_BINS + number]
-                )
-
-        @pl.when(step < blocks - 1)
-        def _():
-            splat(8)
-
-        @pl.when(step == blocks - 1)
-        def _():
-            splat(last)
             for out, begin in ((below, 0), (above, 17)):
-                out[0:META, :] = rec[begin * REC : (begin + GROUP) * REC, :]
                 out[META : META + GROUP, :] = slot_rows[begin : begin + GROUP, :]
                 out[META + GROUP : META + GROUP + 1, :] = code_row[0:1, :]
                 out[META + GROUP + 1 : PAYLOAD, :] = jnp.zeros((6, LANES), jnp.float32)
-            middle[...] = rec[GROUP * REC : 17 * REC, :]
-
-    return call(
-        body,
-        "splat_nbr",
+
+        store_deposits(off, vel, aff, mass, amounts)
+
+        def splat(block, rows):
+            @pl.when(step == block)
+            def _():
+                for row in rows:
+                    number = block * 8 + row
+                    way, index = side_place(number)
+                    out = (below, above)[way]
+                    out[index * REC : (index + 1) * REC, :] = splat_row(
+                        cell, amounts, row, counts[OWN_BINS + number]
+                    )
+
+        for block, rows in enumerate(side_rows):
+            splat(block, rows)
+
+    return call(
+        body,
+        "splat_sides",
         (tile_coords, owner_map, bin_tile, counts, *parts),
         (
-            jax.ShapeDtypeStruct((BINS,), jnp.int32),
+            pltpu.SMEM((BINS,), jnp.int32),
             array(8, LANES),
             array(TPD, LANES),
             array(32, LANES),
             array(PAYLOAD, LANES),
-            array(8 * REC, LANES),
             array(PAYLOAD, LANES),
         ),
-        flops=NBR_BINS * 2_000_000,
-        grid=(blocks,),
-        in_specs=[scalars()] * 4 + particle_specs(first_block),
-        out_specs=(scalars(),) + (held(),) * 6,
-        scratch_shapes=[
-            pltpu.VMEM((NBR_BINS * REC, LANES), jnp.float32),
-            pltpu.VMEM((4, 8, PPT), jnp.float32),
-        ],
+        flops=18 * 2_000_000,
+        grid=(len(side_rows),),
+        in_specs=[scalars()] * 4 + particle_specs(FIRST),
+        out_specs=(scalars(),) + (held(),) * 5,
+        scratch_shapes=[pltpu.VMEM((4, 8, PPT), jnp.float32)],
+    )
+
+
+def splat_middle(counts, slots, parts):
+    def body(counts, slots, cell, off, vel, aff, mass, middle, amounts):
+        store_deposits(off, vel, aff, mass, amounts)
+
+        def splat(block, rows):
+            @pl.when(pl.program_id(0) == block - 1)
+            def _():
+                for row in rows:
+                    number = block * 8 + row
+                    index = number - GROUP
+                    middle[index * REC : (index + 1) * REC, :] = splat_row(
+                        cell, amounts, row, counts[OWN_BINS + number]
+                    )
+
+        for block, rows in middle_rows.items():
+            splat(block, rows)
+
+    return call(
+        body,
+        "splat_middle",
+        (counts, slots, *parts),
+        array(8 * REC, LANES),
+        flops=8 * 2_000_000,
+        grid=(2,),
+        in_specs=[scalars(), scalars()] + particle_specs(FIRST + 1),
+        out_specs=held(),
+        scratch_shapes=[pltpu.VMEM((4, 8, PPT), jnp.float32)],
     )
 
 
@@ -446,7 +486,7 @@
 def project(hot, fluid, velocity, slots, pressure, arrived):
     def body(hot, fluid, velocity, slots, *refs):
         fields = refs[:7]
-        grid_out, tiles, back_p, back_m, back_local, rec = refs[7:]
+        tiles, back_p, back_m, back_local, rec = refs[7:]
         values = fields[0][...]
         ghosts = ghosts_of(hot[...], fields)
         wet = fluid[...] > 0.0
@@ -460,7 +500,6 @@
                 beside(values, ghosts[2 * a], 2 * a) - beside(values, ghosts[2 * a + 1], 2 * a + 1)
             )
             final = jnp.where(wet, velocity[:, a * CELLS : (a + 1) * CELLS] - slope, 0.0)
-            grid_out[a] = final
             copies = pick(named, final)
             for u in range(UPPER):
                 row = a * UPPER + u
@@ -476,7 +515,6 @@
         "project",
         (hot, fluid, velocity, slots, pressure, *arrived),
         (
-            array(3, TPD, CELLS),
             array(TPD * REC, LANES),
             block,
             block,
@@ -486,13 +524,31 @@
     )
 
 
-def sample_row(cell, out, tile, row, count):
-    upper, hot = upper_and_hot(cell, row, count)
+def results(tiles, pressure):
+    def body(tiles, pressure, grid_out, pressure_out):
+        for t in range(TPD):
+            for u in range(UPPER):
+                begin = t * CELLS + u * LANES
+                grid_out[:, begin : begin + LANES] = tiles[pl.ds(t * REC + u, 3, stride=UPPER), :]
+        for u in range(UPPER):
+            pressure_out[pl.ds(u, TPD, stride=UPPER), :] = pressure[:, u * LANES : (u + 1) * LANES]
+
+    return call(
+        body,
+        "results",
+        (tiles, pressure),
+        (array(3, TPD * CELLS), array(TPD * UPPER, LANES)),
+    )
+
+
+def sample_row(cell, tile, row, count):
+    cells = cell[row : row + 1, :]
+    upper = upper_index(cells, LANES, count)
     high = tile.astype(jnp.bfloat16)
     low = (tile - high.astype(jnp.float32)).astype(jnp.bfloat16)
     planes = lax.dot_general(
         jnp.concatenate([high, low], axis=0),
-        hot,
+        one_hot(cells, LANES),
         (((1,), (0,)), ((), ())),
         preferred_element_type=jnp.float32,
     )
@@ -503,9 +559,12 @@
         kept = jnp.where(wanted, planes[8 * half : 8 * half + 8], 0.0)
         kept = kept + pltpu.roll(kept, 7, 0)
         sums.append(kept + pltpu.roll(kept, 6, 0))
-    out[0, row : row + 1, :] = sums[0][0:1]
-    out[1, row : row + 1, :] = sums[0][4:5]
-    out[2, row : row + 1, :] = sums[1][0:1]
+    return sums[0][0:1], sums[0][4:5], sums[1][0:1]
+
+
+def store_row(out, row, values):
+    for a in range(3):
+        out[a, row : row + 1, :] = values[a]
 
 
 particle_shape = jax.ShapeDtypeStruct((3, BINS, PPT), jnp.float32)
@@ -515,10 +574,10 @@
     def body(counts, slots, cell, tiles, *refs):
         out = refs[-1]
         base = (pl.program_id(0) + start) * 8
-
         for row in range(8):
             place = pl.multiple_of(slots[base + row] * REC, REC)
-            sample_row(cell, out, tiles[pl.ds(place, REC), :], row, counts[base + row])
+            tile = tiles[pl.ds(place, REC), :]
+            store_row(out, row, sample_row(cell, tile, row, counts[base + row]))
 
     args = [counts, slots, cell, near(tiles)]
     specs = [
@@ -545,53 +604,79 @@
     )
 
 
-def sample_nbr(counts, cell, buffers, sampled):
-    names = ("xp", "xm", "yp", "ym", "zp", "zm")
-    first_block = OWN_BINS // 8
-    blocks = -(-NBR_BINS // 8)
-
-    def body(counts, cell, *refs):
-        kept = dict(zip(names, refs[:6]))
-        out, rec = refs[7:]
-        step = pl.program_id(0)
-
-        @pl.when(step == 0)
-        def _():
-            for number, source in enumerate(final_sources):
-                rec[number * REC : (number + 1) * REC, :] = record(kept[source[0]], source[1])
-
-        def sample(rows):
-            for row in range(rows):
-                number = step * 8 + row
-                place = pl.multiple_of(number * REC, REC)
-                sample_row(cell, out, rec[pl.ds(place, REC), :], row, counts[OWN_BINS + number])
-
-        @pl.when(step < blocks - 1)
-        def _():
-            sample(8)
-
-        @pl.when(step == blocks - 1)
-        def _():
-            sample(NBR_BINS - 8 * (blocks - 1))
-
-    return call(
-        body,
-        "sample_nbr",
-        (counts, cell, *[near(buffer) for buffer in buffers], sampled),
+def sample_middle(counts, slots, cell, buffers):
+    names = ("yp", "ym", "zp", "zm")
+
+    def body(counts, slots, cell, *refs):
+        held_by = dict(zip(names, refs))
+        out = refs[len(names)]
+
+        def sample(block, rows):
+            @pl.when(pl.program_id(0) == block - 1)
+            def _():
+                for row in rows:
+                    number = block * 8 + row
+                    name, index = final_sources[number]
+                    values = sample_row(
+                        cell, record(held_by[name], index), row, counts[OWN_BINS + number]
+                    )
+                    store_row(out, number - GROUP, values)
+
+        for block, rows in middle_rows.items():
+            sample(block, rows)
+
+    return call(
+        body,
+        "sample_middle",
+        (counts, slots, cell, *[near(buffer) for buffer in buffers]),
+        array(3, 8, PPT),
+        flops=8 * 2_000_000,
+        grid=(2,),
+        in_specs=[scalars(), scalars(), pl.BlockSpec((8, PPT), lambda i: (i + FIRST + 1, 0))]
+        + [held()] * len(names),
+        out_specs=held(),
+    )
+
+
+def sample_sides(counts, cell, buffers, middle, sampled):
+    def body(counts, cell, xp, xm, middle, sampled, out):
+        held_by = {"xp": xp, "xm": xm}
+
+        def sample(block, rows):
+            @pl.when(pl.program_id(0) == block)
+            def _():
+                for row in rows:
+                    number = block * 8 + row
+                    name, index = final_sources[number]
+                    values = sample_row(
+                        cell, record(held_by[name], index), row, counts[OWN_BINS + number]
+                    )
+                    store_row(out, row, values)
+                for row in middle_rows.get(block, ()):
+                    index = block * 8 + row - GROUP
+                    store_row(out, row, [middle[a, index : index + 1, :] for a in range(3)])
+
+        for block, rows in enumerate(side_rows):
+            sample(block, rows)
+
+    return call(
+        body,
+        "sample_sides",
+        (counts, cell, *[near(value) for value in (*buffers, middle)], sampled),
         particle_shape,
-        flops=NBR_BINS * 2_000_000,
-        grid=(blocks,),
-        in_specs=[scalars(), pl.BlockSpec((8, PPT), lambda i: (i + first_block, 0))]
-        + [held()] * 6
+        flops=18 * 2_000_000,
+        grid=(len(side_rows),),
+        in_specs=[scalars(), pl.BlockSpec((8, PPT), lambda i: (i + FIRST, 0))]
+        + [held()] * 3
         + [pl.BlockSpec(memory_space=pl.ANY)],
-        out_specs=pl.BlockSpec((3, 8, PPT), lambda i: (0, i + first_block, 0)),
-        input_output_aliases={8: 0},
-        scratch_shapes=[pltpu.VMEM((NBR_BINS * REC, LANES), jnp.float32)],
+        out_specs=pl.BlockSpec((3, 8, PPT), lambda i: (0, i + FIRST, 0)),
+        input_output_aliases={5: 0},
     )
 
 
 def exchange(values):
-    return [swap(values, axis, which) for axis in AXES for which in (0, 1)]
+    got = {(axis, which): swap(values, axis, which) for which in (0, 1) for axis in AXES}
+    return [got[axis, which] for axis in AXES for which in (0, 1)]
 
 
 def together(*values):
@@ -610,12 +695,11 @@
         jnp.transpose(affine, (1, 0, 2)),
         mass,
     )
-    slots, code_row, code_column, slot_rows, below, middle, above = splat_nbr(
+    slots, code_row, code_column, slot_rows, below, above = splat_sides(
         tile_coords, owner_map, bin_tile, counts, parts
     )
     xp, xm = ring(above, "gx", 1), ring(below, "gx", -1)
-    acc_x = splat_own(counts, slots, parts, 0, 2)
-    xp, xm, acc_x = together(xp, xm, acc_x)
+    middle = splat_middle(counts, slots, parts)
     up, down = forward(
         ("mid", "xp", "xm"),
         (middle, xp, xm),
@@ -626,7 +710,7 @@
     )
     slots, up, down = together(slots, up, down)
     yp, ym = ring(up, "gy", 1), ring(down, "gy", -1)
-    acc_y = splat_own(counts, slots, parts, 2, 1)
+    acc_y = splat_own(counts, slots, parts, 0, 2)
     yp, ym, acc_y = together(yp, ym, acc_y)
     up, down = forward(
         ("mid", "xp", "xm", "yp", "ym"),
@@ -638,15 +722,15 @@
     )
     slots, up, down = together(slots, up, down)
     zp, zm = ring(up, "gz", 1), ring(down, "gz", -1)
-    acc_z = splat_own(counts, slots, parts, 3, 1)
+    acc_z = splat_own(counts, slots, parts, 2, 2)
     arrivals = (xp, xm, yp, ym, zp, zm)
-    grid_u, fluid, nbr_slots = gather_grid(arrivals, (acc_x, acc_y, acc_z))
+    grid_u, fluid, nbr_slots = gather_grid(arrivals, (acc_y, acc_z))
     hot, div, pressure = divergence(
         arrivals, code_row, code_column, grid_u, fluid, exchange(grid_u)
     )
     for _ in range(SWEEPS - 1):
         pressure = sweep(hot, div, fluid, pressure, exchange(pressure))
-    grid_v, tiles, back_p, back_m, kept = project(
+    tiles, back_p, back_m, kept = project(
         hot, fluid, grid_u, nbr_slots, pressure, exchange(pressure)
     )
     rzp, rzm = ring(back_p, "gz", -1), ring(back_m, "gz", 1)
@@ -660,7 +744,7 @@
     )
     slots, up, down = together(slots, up, down)
     ryp, rym = ring(up, "gy", -1), ring(down, "gy", 1)
-    sampled = sample_own(counts, slots, cell, tiles, sampled, 2, 1)
+    sampled = sample_own(counts, slots, cell, tiles, sampled, 2, 2)
     ryp, rym, sampled = together(ryp, rym, sampled)
     up, down = reply(
         ("kept", "zp", "zm", "yp", "ym"),
@@ -670,13 +754,10 @@
     )
     slots, up, down = together(slots, up, down)
     rxp, rxm = ring(up, "gx", -1), ring(down, "gx", 1)
-    sampled = sample_own(counts, slots, cell, tiles, sampled, 3, 1)
-    sampled = sample_nbr(counts, cell, (rxp, rxm, ryp, rym, rzp, rzm), sampled)
-    return (
-        grid_v.reshape(3, TPD * CELLS),
-        pressure.reshape(-1),
-        jnp.transpose(sampled, (1, 0, 2)),
-    )
+    middle = sample_middle(counts, slots, cell, (ryp, rym, rzp, rzm))
+    grid_v, final_pressure = results(tiles, pressure)
+    sampled = sample_sides(counts, cell, (rxp, rxm), middle, sampled)
+    return grid_v, final_pressure.reshape(-1), jnp.transpose(sampled, (1, 0, 2))
 
 
 def solution(mesh):

time: 108 us -> 102 us (0.944)
  Pallas kernels: 34.8 us -> 27.8 us
    pallas_call x18 -> x19, Pallas kernels: 34.8 us -> 27.8 us  [call(): pl.pallas_call(body, out_shape=outs, name=name, cost_estimate=pl.CostEsti...]
  transfers between devices with their start and end apart: 42 -> 42, of which waited for: 12 -> 15; matrix products, arithmetic and copies ran while one was open for 1% -> 1% of each run, Pallas kernels for 18% -> 16%
where the time goes in v2:
time: 102 us; the launch traced here: 101 us
  starting transfers between devices  50.8 us (50%)
  Pallas kernels  27.8 us (27%)
  waiting for transfers between devices  19.9 us (20%)
  local copies, waits for them, and re-layouts  1.27 us (1%)
    ppermute x30, starting transfers between devices, swap(): return lax.ppermute(block, axis, [(i, j % size) for i, j in pairs])  33.4 us
    pallas_call x19, Pallas kernels, call(): pl.pallas_call(body, out_shape=outs, name=name, cost_estimate=pl.CostEsti...  27.8 us
    ppermute x12, starting transfers between devices, ring(): lax.ppermute(block, axis, [(i, (i + distance) % size) for i in range(size)])  17.3 us
    ppermute x30, waiting for transfers between devices, swap(): return lax.ppermute(block, axis, [(i, j % size) for i, j in pairs])  16.8 us
    ppermute x12, waiting for transfers between devices, ring(): lax.ppermute(block, axis, [(i, (i + distance) % size) for i in range(size)])  3.15 us
  transfers between devices with their start and end apart: 42, of which 15 were waited for; matrix products, arithmetic and copies ran while one was open for 1% of the time, Pallas kernels for 16%

profile of v2, /device:TPU:1, one launch (start us, length us, event | category | flops | bytes accessed | tf_op | source)
XLA Modules:
  0.0 100.7 jit_solution(9973433906763813106)
XLA Ops:
  0.6 4.7 %splat_sides.1 = (s32[58]{0:T(128)S(4)}, f32[8,128]{1,0:T(8,128)S(1)}, f32[16,128]{1,0:T(8,128)S(1)}, f32[32,128]{1,0:T(8,128)S(1)}, f32[160,128]{1,0:T(8,128)S(1)}, /*index=5*/f32[160,128]{1,0:T(8,128)S(1)}) custom-call(s32[3,16]{1,0:T(4,128)} %coords.1, s32[4096]{0:T(1024)} %owners.1, s32[58]{0:T(128)} %bin_tile.1, s32[58]{0:T(128)} %counts.15, ...), custom_call_target="tpu_custom_call" | custom-call | flops 36000000 | bytes 500000 | tf_op jit(solution)/shard_map/splat_sides/pallas_call | solution.py:57
  5.4 2.1 %collective-permute-start = (f32[160,128]{1,0:T(8,128)S(1)}, f32[160,128]{1,0:T(8,128)S(1)}, u32[]{:S(2)}, u32[]{:S(2)}) collective-permute-start(f32[160,128]{1,0:T(8,128)S(1)} %get-tuple-element.50), channel_id=1, source_target_pairs={{0,64},{64,128},{128,192},{192,0},{1,65},{65,129},{129,193},{193,1... | collective-permute-start | bytes 245768 | tf_op jit(solution)/shard_map/ppermute | solution.py:27
  8.8 2.4 %splat_middle.1.refs_0_ = f32[128,128]{1,0:T(8,128)S(1)} custom-call(s32[58]{0:T(128)} %counts.15, s32[58]{0:T(128)S(4)} %get-tuple-element.95.slots, s32[58,2048]{1,0:T(8,128)} %cell.15, f32[3,58,2048]{2,1,0:T(8,128)} %bitcast.11, f32[3,58,2048]{2,1,0:T(8,128)} %bitcast.15, f32[9,58,2048]{2,1,0:T(8,128)} %bitcast.7, f32[58,2048]{1,0:T(8,128)} %mass.7), custom_call_target="tpu_custom_call" | custom-call | flops 16000000 | bytes 500000 | tf_op jit(solution)/shard_map/splat_middle/pallas_call | solution.py:57
  11.2 1.8 %collective-permute-start.2 = (f32[160,128]{1,0:T(8,128)S(1)}, f32[160,128]{1,0:T(8,128)S(1)}, u32[]{:S(2)}, u32[]{:S(2)}) collective-permute-start(f32[160,128]{1,0:T(8,128)S(1)} %get-tuple-element.57), channel_id=1, source_target_pairs={{0,8},{8,16},{16,24},{24,32},{32,40},{40,48},{48,56},{56,0},{1,9},... | collective-permute-start | bytes 245768 | tf_op jit(solution)/shard_map/ppermute | solution.py:27
  13.1 4.0 %collective-permute-start.3 = (f32[160,128]{1,0:T(8,128)S(1)}, f32[160,128]{1,0:T(8,128)S(1)}, u32[]{:S(2)}, u32[]{:S(2)}) collective-permute-start(f32[160,128]{1,0:T(8,128)S(1)} %get-tuple-element.58), channel_id=1, source_target_pairs={{0,56},{8,0},{16,8},{24,16},{32,24},{40,32},{48,40},{56,48},{1,57}... | collective-permute-start | bytes 245768 | tf_op jit(solution)/shard_map/ppermute | solution.py:27
  17.1 2.9 %splat_own.2.refs_6_ = f32[256,128]{1,0:T(8,128)S(1)} custom-call(s32[58]{0:T(128)} %counts.15, s32[58]{0:T(128)S(4)} %get-tuple-element.95.slots, s32[58,2048]{1,0:T(8,128)} %cell.15, f32[3,58,2048]{2,1,0:T(8,128)} %bitcast.12, f32[3,58,2048]{2,1,0:T(8,128)} %bitcast.16, f32[9,58,2048]{2,1,0:T(8,128)} %bitcast.8, f32[58,2048]{1,0:T(8,128)} %mass.7), custom_call_target="tpu_custom_call" | custom-call | flops 32000000 | bytes 500000 | tf_op jit(solution)/shard_map/splat_own/pallas_call | solution.py:57
  20.1 3.0 %collective-permute-start.4 = (f32[160,128]{1,0:T(8,128)S(1)}, f32[160,128]{1,0:T(8,128)S(1)}, u32[]{:S(2)}, u32[]{:S(2)}) collective-permute-start(f32[160,128]{1,0:T(8,128)S(1)} %get-tuple-element.64), channel_id=1, source_target_pairs={{0,1},{1,2},{2,3},{3,4},{4,5},{5,6},{6,7},{7,0},{8,9},{9,10},{10,1... | collective-permute-start | bytes 245768 | tf_op jit(solution)/shard_map/ppermute | solution.py:27
  23.1 2.9 %splat_own.3.refs_7_ = f32[256,128]{1,0:T(8,128)S(1)} custom-call(s32[58]{0:T(128)} %counts.15, s32[58]{0:T(128)S(4)} %get-tuple-element.95.slots, s32[58,2048]{1,0:T(8,128)} %cell.15, f32[3,58,2048]{2,1,0:T(8,128)} %bitcast.13, f32[3,58,2048]{2,1,0:T(8,128)} %bitcast.17, f32[9,58,2048]{2,1,0:T(8,128)} %bitcast.9, f32[58,2048]{1,0:T(8,128)} %mass.7), custom_call_target="tpu_custom_call" | custom-call | flops 32000000 | bytes 500000 | tf_op jit(solution)/shard_map/splat_own/pallas_call | solution.py:57
  31.8 2.9 %collective-permute-start.9 = (f32[16,1536]{1,0:T(8,128)S(1)}, f32[16,1536]{1,0:T(8,128)S(1)}, u32[]{:S(2)}, u32[]{:S(2)}) collective-permute-start(f32[16,1536]{1,0:T(8,128)S(1)} %get-tuple-element.70.refs_9_.velocity), channel_id=1, source_target_pairs={{0,56},{8,16},{16,8},{24,32},{32,24},{40,48},{48,40},{56,0},{1,57}... | collective-permute-start | bytes 294920 | tf_op jit(solution)/shard_map/ppermute | solution.py:33
  38.7 1.8 %collective-permute-start.14 = (f32[16,512]{1,0:T(8,128)S(1)}, f32[16,512]{1,0:T(8,128)S(1)}, u32[]{:S(2)}, u32[]{:S(2)}) collective-permute-start(f32[16,512]{1,0:T(8,128)S(1)} %get-tuple-element.74.refs_0_), channel_id=1, source_target_pairs={{0,8},{8,0},{16,24},{24,16},{32,40},{40,32},{48,56},{56,48},{1,9},... | collective-permute-start | bytes 98312 | tf_op jit(solution)/shard_map/ppermute | solution.py:33
  41.4 3.9 %collective-permute-start.16 = (f32[16,512]{1,0:T(8,128)S(1)}, f32[16,512]{1,0:T(8,128)S(1)}, u32[]{:S(2)}, u32[]{:S(2)}) collective-permute-start(f32[16,512]{1,0:T(8,128)S(1)} %get-tuple-element.74.refs_0_), channel_id=1, source_target_pairs={{0,1},{1,0},{2,3},{3,2},{4,5},{5,4},{6,7},{7,6},{8,9},{9,8},{10,11... | collective-permute-start | bytes 98312 | tf_op jit(solution)/shard_map/ppermute | solution.py:33
  46.1 2.8 %collective-permute-done.17.refs_6_ = f32[16,512]{1,0:T(8,128)S(1)} collective-permute-done((f32[16,512]{1,0:T(8,128)S(1)}, f32[16,512]{1,0:T(8,128)S(1)}, u32[]{:S(2)}, u32[]{:S(2)}) %collective-permute-start.17) | collective-permute-done | bytes 32800 | tf_op jit(solution)/shard_map/ppermute | solution.py:33
  51.8 1.8 %collective-permute-start.20 = (f32[16,512]{1,0:T(8,128)S(1)}, f32[16,512]{1,0:T(8,128)S(1)}, u32[]{:S(2)}, u32[]{:S(2)}) collective-permute-start(f32[16,512]{1,0:T(8,128)S(1)} %sweep.3.refs_0_), channel_id=1, source_target_pairs={{0,8},{8,0},{16,24},{24,16},{32,40},{40,32},{48,56},{56,48},{1,9},... | collective-permute-start | bytes 98312 | tf_op jit(solution)/shard_map/ppermute | solution.py:33
  54.2 2.0 %collective-permute-start.22 = (f32[16,512]{1,0:T(8,128)S(1)}, f32[16,512]{1,0:T(8,128)S(1)}, u32[]{:S(2)}, u32[]{:S(2)}) collective-permute-start(f32[16,512]{1,0:T(8,128)S(1)} %sweep.3.refs_0_), channel_id=1, source_target_pairs={{0,1},{1,0},{2,3},{3,2},{4,5},{5,4},{6,7},{7,6},{8,9},{9,8},{10,11... | collective-permute-start | bytes 98312 | tf_op jit(solution)/shard_map/ppermute | solution.py:33
  57.6 2.2 %collective-permute-done.23.refs_6_ = f32[16,512]{1,0:T(8,128)S(1)} collective-permute-done((f32[16,512]{1,0:T(8,128)S(1)}, f32[16,512]{1,0:T(8,128)S(1)}, u32[]{:S(2)}, u32[]{:S(2)}) %collective-permute-start.23) | collective-permute-done | bytes 32800 | tf_op jit(solution)/shard_map/ppermute | solution.py:33
  64.2 1.9 %collective-permute-start.28 = (f32[16,512]{1,0:T(8,128)S(1)}, f32[16,512]{1,0:T(8,128)S(1)}, u32[]{:S(2)}, u32[]{:S(2)}) collective-permute-start(f32[16,512]{1,0:T(8,128)S(1)} %sweep.4.refs_0_), channel_id=1, source_target_pairs={{0,1},{1,0},{2,3},{3,2},{4,5},{5,4},{6,7},{7,6},{8,9},{9,8},{10,11... | collective-permute-start | bytes 98312 | tf_op jit(solution)/shard_map/ppermute | solution.py:33
  67.0 2.8 %collective-permute-done.29.refs_6_ = f32[16,512]{1,0:T(8,128)S(1)} collective-permute-done((f32[16,512]{1,0:T(8,128)S(1)}, f32[16,512]{1,0:T(8,128)S(1)}, u32[]{:S(2)}, u32[]{:S(2)}) %collective-permute-start.29) | collective-permute-done | bytes 32800 | tf_op jit(solution)/shard_map/ppermute | solution.py:33
  73.4 2.0 %collective-permute-start.34 = (f32[16,512]{1,0:T(8,128)S(1)}, f32[16,512]{1,0:T(8,128)S(1)}, u32[]{:S(2)}, u32[]{:S(2)}) collective-permute-start(f32[16,512]{1,0:T(8,128)S(1)} %sweep.5.refs_0_.pressure), channel_id=1, source_target_pairs={{0,1},{1,0},{2,3},{3,2},{4,5},{5,4},{6,7},{7,6},{8,9},{9,8},{10,11... | collective-permute-start | bytes 98312 | tf_op jit(solution)/shard_map/ppermute | solution.py:33
  76.9 2.1 %collective-permute-done.35.refs_6_ = f32[16,512]{1,0:T(8,128)S(1)} collective-permute-done((f32[16,512]{1,0:T(8,128)S(1)}, f32[16,512]{1,0:T(8,128)S(1)}, u32[]{:S(2)}, u32[]{:S(2)}) %collective-permute-start.35) | collective-permute-done | bytes 32800 | tf_op jit(solution)/shard_map/ppermute | solution.py:33
  81.4 3.1 %sample_own.2.refs_0_ = f32[3,58,2048]{2,1,0:T(8,128)} custom-call(s32[58]{0:T(128)} %counts.15, s32[58]{0:T(128)S(4)} %get-tuple-element.95.slots, s32[58,2048]{1,0:T(8,128)} %cell.15, f32[256,128]{1,0:T(8,128)S(1)} %get-tuple-element.75.tiles), custom_call_target="tpu_custom_call" | custom-call | flops 32000000 | bytes 500000 | tf_op jit(solution)/shard_map/sample_own/pallas_call | solution.py:57
  84.5 1.7 %collective-permute-start.38 = (f32[144,128]{1,0:T(8,128)S(1)}, f32[144,128]{1,0:T(8,128)S(1)}, u32[]{:S(2)}, u32[]{:S(2)}) collective-permute-start(f32[144,128]{1,0:T(8,128)S(1)} %get-tuple-element.86), channel_id=1, source_target_pairs={{0,56},{8,0},{16,8},{24,16},{32,24},{40,32},{48,40},{56,48},{1,57}... | collective-permute-start | bytes 221192 | tf_op jit(solution)/shard_map/ppermute | solution.py:27
  86.3 3.2 %sample_own.3.sampled = f32[3,58,2048]{2,1,0:T(8,128)} custom-call(s32[58]{0:T(128)} %counts.15, s32[58]{0:T(128)S(4)} %get-tuple-element.95.slots, s32[58,2048]{1,0:T(8,128)} %cell.15, f32[256,128]{1,0:T(8,128)S(1)} %get-tuple-element.75.tiles, f32[3,58,2048]{2,1,0:T(8,128)} %sample_own.2.refs_0_), custom_call_target="tpu_custom_call", output_to_operand_aliasing={{}: (4, {})} | custom-call | flops 32000000 | bytes 500000 | tf_op jit(solution)/shard_map/sample_own/pallas_call | solution.py:57
  93.5 1.8 %sample_middle.1.middle = f32[3,8,2048]{2,1,0:T(8,128)S(1)} custom-call(s32[58]{0:T(128)} %counts.15, s32[58]{0:T(128)S(4)} %get-tuple-element.95.slots, s32[58,2048]{1,0:T(8,128)} %cell.15, f32[144,128]{1,0:T(8,128)S(1)} %collective-permute-done.38.refs_3_.refs_0_, f32[144,128]{1,0:T(8,128)S(1)} %collective-permute-done.39.refs_4_.refs_1_, ...), custom_call_target="tpu_custom_call" | custom-call | flops 16000000 | bytes 500000 | tf_op jit(solution)/shard_map/sample_middle/pallas_call | solution.py:57
  96.3 4.3 %sample_sides.1 = f32[3,58,2048]{2,1,0:T(8,128)} custom-call(s32[58]{0:T(128)} %counts.15, s32[58,2048]{1,0:T(8,128)} %cell.15, f32[144,128]{1,0:T(8,128)S(1)} %collective-permute-done.40.xp, f32[144,128]{1,0:T(8,128)S(1)} %collective-permute-done.41.xm, f32[3,8,2048]{2,1,0:T(8,128)S(1)} %sample_middle.1.middle, ...), custom_call_target="tpu_custom_call", output_to_operand_aliasing={{}: (5, {})} | custom-call | flops 36000000 | bytes 500000 | tf_op jit(solution)/shard_map/sample_sides/pallas_call | solution.py:57
  (81 shorter events, 35.5 us)
Async XLA Ops:
  5.4 5.8 %collective-permute-start = (f32[160,128]{1,0:T(8,128)S(1)}, f32[160,128]{1,0:T(8,128)S(1)}, u32[]{:S(2)}, u32[]{:S(2)}) collective-permute-start(f32[160,128]{1,0:T(8,128)S(1)} %get-tuple-element.50), channel_id=1, source_target_pairs={{0,64},{64,128},{128,192},{192,0},{1,65},{65,129},{129,193},{193,1... | collective-permute-start | bytes 245768 | tf_op jit(solution)/shard_map/ppermute | solution.py:27
  11.2 8.8 %collective-permute-start.2 = (f32[160,128]{1,0:T(8,128)S(1)}, f32[160,128]{1,0:T(8,128)S(1)}, u32[]{:S(2)}, u32[]{:S(2)}) collective-permute-start(f32[160,128]{1,0:T(8,128)S(1)} %get-tuple-element.57), channel_id=1, source_target_pairs={{0,8},{8,16},{16,24},{24,32},{32,40},{40,48},{48,56},{56,0},{1,9},... | collective-permute-start | bytes 245768 | tf_op jit(solution)/shard_map/ppermute | solution.py:27
  13.1 7.0 %collective-permute-start.3 = (f32[160,128]{1,0:T(8,128)S(1)}, f32[160,128]{1,0:T(8,128)S(1)}, u32[]{:S(2)}, u32[]{:S(2)}) collective-permute-start(f32[160,128]{1,0:T(8,128)S(1)} %get-tuple-element.58), channel_id=1, source_target_pairs={{0,56},{8,0},{16,8},{24,16},{32,24},{40,32},{48,40},{56,48},{1,57}... | collective-permute-start | bytes 245768 | tf_op jit(solution)/shard_map/ppermute | solution.py:27
  20.1 5.9 %collective-permute-start.4 = (f32[160,128]{1,0:T(8,128)S(1)}, f32[160,128]{1,0:T(8,128)S(1)}, u32[]{:S(2)}, u32[]{:S(2)}) collective-permute-start(f32[160,128]{1,0:T(8,128)S(1)} %get-tuple-element.64), channel_id=1, source_target_pairs={{0,1},{1,2},{2,3},{3,4},{4,5},{5,6},{6,7},{7,0},{8,9},{9,10},{10,1... | collective-permute-start | bytes 245768 | tf_op jit(solution)/shard_map/ppermute | solution.py:27
  27.3 4.5 %collective-permute-start.10 = (f32[16,1536]{1,0:T(8,128)S(1)}, f32[16,1536]{1,0:T(8,128)S(1)}, u32[]{:S(2)}, u32[]{:S(2)}) collective-permute-start(f32[16,1536]{1,0:T(8,128)S(1)} %get-tuple-element.70.refs_9_.velocity), channel_id=1, source_target_pairs={{0,1},{1,0},{2,3},{3,2},{4,5},{5,4},{6,7},{7,6},{8,9},{9,8},{10,11... | collective-permute-start | bytes 294920 | tf_op jit(solution)/shard_map/ppermute | solution.py:33
  28.2 6.4 %collective-permute-start.11 = (f32[16,1536]{1,0:T(8,128)S(1)}, f32[16,1536]{1,0:T(8,128)S(1)}, u32[]{:S(2)}, u32[]{:S(2)}) collective-permute-start(f32[16,1536]{1,0:T(8,128)S(1)} %get-tuple-element.70.refs_9_.velocity), channel_id=1, source_target_pairs={{0,7},{1,2},{2,1},{3,4},{4,3},{5,6},{6,5},{7,0},{8,15},{9,10},{10,... | collective-permute-start | bytes 294920 | tf_op jit(solution)/shard_map/ppermute | solution.py:33
  29.0 5.6 %collective-permute-start.6 = (f32[16,1536]{1,0:T(8,128)S(1)}, f32[16,1536]{1,0:T(8,128)S(1)}, u32[]{:S(2)}, u32[]{:S(2)}) collective-permute-start(f32[16,1536]{1,0:T(8,128)S(1)} %get-tuple-element.70.refs_9_.velocity), channel_id=1, source_target_pairs={{0,64},{64,0},{128,192},{192,128},{1,65},{65,1},{129,193},{193,129... | collective-permute-start | bytes 294920 | tf_op jit(solution)/shard_map/ppermute | solution.py:33
  30.2 4.7 %collective-permute-start.7 = (f32[16,1536]{1,0:T(8,128)S(1)}, f32[16,1536]{1,0:T(8,128)S(1)}, u32[]{:S(2)}, u32[]{:S(2)}) collective-permute-start(f32[16,1536]{1,0:T(8,128)S(1)} %get-tuple-element.70.refs_9_.velocity), channel_id=1, source_target_pairs={{0,192},{64,128},{128,64},{192,0},{1,193},{65,129},{129,65},{193,1... | collective-permute-start | bytes 294920 | tf_op jit(solution)/shard_map/ppermute | solution.py:33
  31.8 5.2 %collective-permute-start.9 = (f32[16,1536]{1,0:T(8,128)S(1)}, f32[16,1536]{1,0:T(8,128)S(1)}, u32[]{:S(2)}, u32[]{:S(2)}) collective-permute-start(f32[16,1536]{1,0:T(8,128)S(1)} %get-tuple-element.70.refs_9_.velocity), channel_id=1, source_target_pairs={{0,56},{8,16},{16,8},{24,32},{32,24},{40,48},{48,40},{56,0},{1,57}... | collective-permute-start | bytes 294920 | tf_op jit(solution)/shard_map/ppermute | solution.py:33
  37.4 7.9 %collective-permute-start.12 = (f32[16,512]{1,0:T(8,128)S(1)}, f32[16,512]{1,0:T(8,128)S(1)}, u32[]{:S(2)}, u32[]{:S(2)}) collective-permute-start(f32[16,512]{1,0:T(8,128)S(1)} %get-tuple-element.74.refs_0_), channel_id=1, source_target_pairs={{0,64},{64,0},{128,192},{192,128},{1,65},{65,1},{129,193},{193,129... | collective-permute-start | bytes 98312 | tf_op jit(solution)/shard_map/ppermute | solution.py:33
  38.0 7.3 %collective-permute-start.13 = (f32[16,512]{1,0:T(8,128)S(1)}, f32[16,512]{1,0:T(8,128)S(1)}, u32[]{:S(2)}, u32[]{:S(2)}) collective-permute-start(f32[16,512]{1,0:T(8,128)S(1)} %get-tuple-element.74.refs_0_), channel_id=1, source_target_pairs={{0,192},{64,128},{128,64},{192,0},{1,193},{65,129},{129,65},{193,1... | collective-permute-start | bytes 98312 | tf_op jit(solution)/shard_map/ppermute | solution.py:33
  38.7 6.6 %collective-permute-start.14 = (f32[16,512]{1,0:T(8,128)S(1)}, f32[16,512]{1,0:T(8,128)S(1)}, u32[]{:S(2)}, u32[]{:S(2)}) collective-permute-start(f32[16,512]{1,0:T(8,128)S(1)} %get-tuple-element.74.refs_0_), channel_id=1, source_target_pairs={{0,8},{8,0},{16,24},{24,16},{32,40},{40,32},{48,56},{56,48},{1,9},... | collective-permute-start | bytes 98312 | tf_op jit(solution)/shard_map/ppermute | solution.py:33
  40.5 4.8 %collective-permute-start.15 = (f32[16,512]{1,0:T(8,128)S(1)}, f32[16,512]{1,0:T(8,128)S(1)}, u32[]{:S(2)}, u32[]{:S(2)}) collective-permute-start(f32[16,512]{1,0:T(8,128)S(1)} %get-tuple-element.74.refs_0_), channel_id=1, source_target_pairs={{0,56},{8,16},{16,8},{24,32},{32,24},{40,48},{48,40},{56,0},{1,57}... | collective-permute-start | bytes 98312 | tf_op jit(solution)/shard_map/ppermute | solution.py:33
  41.4 4.8 %collective-permute-start.16 = (f32[16,512]{1,0:T(8,128)S(1)}, f32[16,512]{1,0:T(8,128)S(1)}, u32[]{:S(2)}, u32[]{:S(2)}) collective-permute-start(f32[16,512]{1,0:T(8,128)S(1)} %get-tuple-element.74.refs_0_), channel_id=1, source_target_pairs={{0,1},{1,0},{2,3},{3,2},{4,5},{5,4},{6,7},{7,6},{8,9},{9,8},{10,11... | collective-permute-start | bytes 98312 | tf_op jit(solution)/shard_map/ppermute | solution.py:33
  49.3 6.9 %collective-permute-start.18 = (f32[16,512]{1,0:T(8,128)S(1)}, f32[16,512]{1,0:T(8,128)S(1)}, u32[]{:S(2)}, u32[]{:S(2)}) collective-permute-start(f32[16,512]{1,0:T(8,128)S(1)} %sweep.3.refs_0_), channel_id=1, source_target_pairs={{0,64},{64,0},{128,192},{192,128},{1,65},{65,1},{129,193},{193,129... | collective-permute-start | bytes 98312 | tf_op jit(solution)/shard_map/ppermute | solution.py:33
  50.2 6.0 %collective-permute-start.19 = (f32[16,512]{1,0:T(8,128)S(1)}, f32[16,512]{1,0:T(8,128)S(1)}, u32[]{:S(2)}, u32[]{:S(2)}) collective-permute-start(f32[16,512]{1,0:T(8,128)S(1)} %sweep.3.refs_0_), channel_id=1, source_target_pairs={{0,192},{64,128},{128,64},{192,0},{1,193},{65,129},{129,65},{193,1... | collective-permute-start | bytes 98312 | tf_op jit(solution)/shard_map/ppermute | solution.py:33
  60.2 5.9 %collective-permute-start.24 = (f32[16,512]{1,0:T(8,128)S(1)}, f32[16,512]{1,0:T(8,128)S(1)}, u32[]{:S(2)}, u32[]{:S(2)}) collective-permute-start(f32[16,512]{1,0:T(8,128)S(1)} %sweep.4.refs_0_), channel_id=1, source_target_pairs={{0,64},{64,0},{128,192},{192,128},{1,65},{65,1},{129,193},{193,129... | collective-permute-start | bytes 98312 | tf_op jit(solution)/shard_map/ppermute | solution.py:33
  61.1 5.0 %collective-permute-start.25 = (f32[16,512]{1,0:T(8,128)S(1)}, f32[16,512]{1,0:T(8,128)S(1)}, u32[]{:S(2)}, u32[]{:S(2)}) collective-permute-start(f32[16,512]{1,0:T(8,128)S(1)} %sweep.4.refs_0_), channel_id=1, source_target_pairs={{0,192},{64,128},{128,64},{192,0},{1,193},{65,129},{129,65},{193,1... | collective-permute-start | bytes 98312 | tf_op jit(solution)/shard_map/ppermute | solution.py:33
  61.5 4.6 %collective-permute-start.26 = (f32[16,512]{1,0:T(8,128)S(1)}, f32[16,512]{1,0:T(8,128)S(1)}, u32[]{:S(2)}, u32[]{:S(2)}) collective-permute-start(f32[16,512]{1,0:T(8,128)S(1)} %sweep.4.refs_0_), channel_id=1, source_target_pairs={{0,8},{8,0},{16,24},{24,16},{32,40},{40,32},{48,56},{56,48},{1,9},... | collective-permute-start | bytes 98312 | tf_op jit(solution)/shard_map/ppermute | solution.py:33
  70.1 5.3 %collective-permute-start.30 = (f32[16,512]{1,0:T(8,128)S(1)}, f32[16,512]{1,0:T(8,128)S(1)}, u32[]{:S(2)}, u32[]{:S(2)}) collective-permute-start(f32[16,512]{1,0:T(8,128)S(1)} %sweep.5.refs_0_.pressure), channel_id=1, source_target_pairs={{0,64},{64,0},{128,192},{192,128},{1,65},{65,1},{129,193},{193,129... | collective-permute-start | bytes 98312 | tf_op jit(solution)/shard_map/ppermute | solution.py:33
  79.6 4.9 %collective-permute-start.36 = (f32[144,128]{1,0:T(8,128)S(1)}, f32[144,128]{1,0:T(8,128)S(1)}, u32[]{:S(2)}, u32[]{:S(2)}) collective-permute-start(f32[144,128]{1,0:T(8,128)S(1)} %get-tuple-element.79), channel_id=1, source_target_pairs={{0,7},{1,0},{2,1},{3,2},{4,3},{5,4},{6,5},{7,6},{8,15},{9,8},{10,9... | collective-permute-start | bytes 221192 | tf_op jit(solution)/shard_map/ppermute | solution.py:27
  84.5 4.9 %collective-permute-start.38 = (f32[144,128]{1,0:T(8,128)S(1)}, f32[144,128]{1,0:T(8,128)S(1)}, u32[]{:S(2)}, u32[]{:S(2)}) collective-permute-start(f32[144,128]{1,0:T(8,128)S(1)} %get-tuple-element.86), channel_id=1, source_target_pairs={{0,56},{8,0},{16,8},{24,16},{32,24},{40,32},{48,40},{56,48},{1,57}... | collective-permute-start | bytes 221192 | tf_op jit(solution)/shard_map/ppermute | solution.py:27
  86.3 4.4 %collective-permute-start.39 = (f32[144,128]{1,0:T(8,128)S(1)}, f32[144,128]{1,0:T(8,128)S(1)}, u32[]{:S(2)}, u32[]{:S(2)}) collective-permute-start(f32[144,128]{1,0:T(8,128)S(1)} %get-tuple-element.87), channel_id=1, source_target_pairs={{0,8},{8,16},{16,24},{24,32},{32,40},{40,48},{48,56},{56,0},{1,9},... | collective-permute-start | bytes 221192 | tf_op jit(solution)/shard_map/ppermute | solution.py:27
  90.7 4.7 %collective-permute-start.40 = (f32[144,128]{1,0:T(8,128)S(1)}, f32[144,128]{1,0:T(8,128)S(1)}, u32[]{:S(2)}, u32[]{:S(2)}) collective-permute-start(f32[144,128]{1,0:T(8,128)S(1)} %get-tuple-element.93), channel_id=1, source_target_pairs={{0,192},{64,0},{128,64},{192,128},{1,193},{65,1},{129,65},{193,129... | collective-permute-start | bytes 221192 | tf_op jit(solution)/shard_map/ppermute | solution.py:27
  (18 other events, 67.8 us)
